TPU v7x, 8 devices: a whole 2x2x1 slice. The times are simulated.
8 devices in a mesh: dp: 1 (over z), stage: 8 (over y, x, core).
Axes of the slice: x: 2, y: 2, z: 1, core: 2. Of those that a mesh axis runs over, the one named last changes fastest.
Arguments:
- tokens_in: bfloat16 [4, 1024, 1280], P('dp')
- targets: bfloat16 [4, 1024, 1280], P('dp')
- w_in: bfloat16 [16, 1280, 5120], P('stage')
- w_out: bfloat16 [16, 5120, 1280], P('stage')
- norm_gains: float32 [16, 1280], P('stage')
Outputs:
- output 1: float32 [16, 1280, 5120], P(('dp', 'stage'))
- output 2: float32 [16, 5120, 1280], P(('dp', 'stage'))
- output 3: float32 [16, 1280], P(('dp', 'stage'))
- output 4: float32 [1], P('dp')
All inputs are finite; a program needn't handle non-finite values.
Results may differ from a plain program's by a relative error of at most 0.00522216.
Values are sent between devices in bfloat16 or wider.
A program may use at most 1 GiB of HBM per device.

v0:
```python
import jax
import jax.numpy as jnp
from jax import lax
from jax.sharding import PartitionSpec as P

EPSILON = 1e-6


def norm_scale(x_f32, gain_vec):
    inv_rms = lax.rsqrt(jnp.mean(x_f32 * x_f32, axis=-1, keepdims=True) + EPSILON)
    return x_f32 * inv_rms * gain_vec


def layer_forward(x_act, first_w, second_w, gain_vec):
    x_f32 = x_act.astype(jnp.float32)
    normed = norm_scale(x_f32, gain_vec).astype(jnp.bfloat16)
    pre_act = jnp.dot(normed, first_w, preferred_element_type=jnp.float32)
    hidden = jax.nn.gelu(pre_act).astype(jnp.bfloat16)
    out_f32 = jnp.dot(hidden, second_w, preferred_element_type=jnp.float32)
    return (x_f32 + out_f32).astype(jnp.bfloat16)


def layer_backward(x_act, grad_h, first_w, second_w, gain_vec):
    x_f32 = x_act.astype(jnp.float32)
    normed_f32, norm_vjp = jax.vjp(norm_scale, x_f32, gain_vec)
    normed = normed_f32.astype(jnp.bfloat16)
    pre_act = jnp.dot(normed, first_w, preferred_element_type=jnp.float32)
    hidden_f32, gelu_vjp = jax.vjp(jax.nn.gelu, pre_act)
    hidden = hidden_f32.astype(jnp.bfloat16)
    grad_second = jnp.einsum('tf,td->fd', hidden, grad_h, preferred_element_type=jnp.float32)
    grad_hidden = jnp.einsum('td,fd->tf', grad_h, second_w, preferred_element_type=jnp.float32)
    grad_pre = gelu_vjp(grad_hidden)[0].astype(jnp.bfloat16)
    grad_first = jnp.einsum('td,tf->df', normed, grad_pre, preferred_element_type=jnp.float32)
    grad_normed = jnp.einsum('tf,df->td', grad_pre, first_w, preferred_element_type=jnp.float32)
    grad_x_norm, grad_gain = norm_vjp(grad_normed)
    grad_x = (grad_h.astype(jnp.float32) + grad_x_norm).astype(jnp.bfloat16)
    return grad_x, grad_first, grad_second, grad_gain


def segment_forward(x_act, first_w, second_w, gain_rows):
    kept_list = []
    for layer_idx in range(first_w.shape[0]):
        kept_list.append(x_act)
        x_act = layer_forward(x_act, first_w[layer_idx], second_w[layer_idx], gain_rows[layer_idx])
    return x_act, jnp.stack(kept_list)


def segment_backward(kept_inputs, grad_h, first_w, second_w, gain_rows, grad_sums):
    layer_count = first_w.shape[0]
    first_list = [None] * layer_count
    second_list = [None] * layer_count
    gain_list = [None] * layer_count
    for layer_idx in reversed(range(layer_count)):
        grad_h, grad_first, grad_second, grad_gain = layer_backward(
            kept_inputs[layer_idx], grad_h, first_w[layer_idx], second_w[layer_idx], gain_rows[layer_idx])
        first_list[layer_idx] = grad_first
        second_list[layer_idx] = grad_second
        gain_list[layer_idx] = grad_gain
    new_sums = (grad_sums[0] + jnp.stack(first_list), grad_sums[1] + jnp.stack(second_list),
                grad_sums[2] + jnp.stack(gain_list))
    return grad_h, new_sums


def store_inputs(buffer_all, kept_inputs, mb_index, is_valid):
    old_rows = lax.dynamic_index_in_dim(buffer_all, mb_index, 1, keepdims=False)
    return lax.dynamic_update_index_in_dim(buffer_all, jnp.where(is_valid, kept_inputs, old_rows), mb_index, 1)


def solution(mesh):
    stages = mesh.shape['stage']
    down_perm = [(src_idx, src_idx + 1) for src_idx in range(stages - 1)]
    up_perm = [(src_idx + 1, src_idx) for src_idx in range(stages - 1)]

    def device_step(tokens, targets, w_in, w_out, norm_gains):
        stage_idx = lax.axis_index('stage')
        micro_count, tokens_mb, d_model = tokens.shape
        d_ff = w_in.shape[2]
        segment = w_in.shape[0] // 2
        tick_count = micro_count + 2 * stages - 1
        is_first = stage_idx == 0
        is_last = stage_idx == stages - 1
        up_offset = 2 * stages - 1 - stage_idx
        down_weights = (w_in[:segment], w_out[:segment], norm_gains[:segment])
        up_weights = (w_in[segment:], w_out[segment:], norm_gains[segment:])
        zero_act = jnp.zeros((tokens_mb, d_model), jnp.bfloat16)
        zero_saved = jnp.zeros((segment,) + tokens.shape, jnp.bfloat16)

        def run_down(x_act):
            return segment_forward(x_act, down_weights[0], down_weights[1], down_weights[2])

        def run_up(x_act):
            return segment_forward(x_act, up_weights[0], up_weights[1], up_weights[2])

        def skip_forward(x_act):
            return x_act, jnp.zeros((segment, tokens_mb, d_model), jnp.bfloat16)

        def forward_tick(loop_state, tick_idx):
            in_down, in_up, saved_down, saved_up, finals = loop_state
            mb_down = tick_idx - stage_idx
            mb_up = tick_idx - up_offset
            ok_down = (mb_down >= 0) & (mb_down < micro_count)
            ok_up = (mb_up >= 0) & (mb_up < micro_count)
            idx_down = jnp.clip(mb_down, 0, micro_count - 1)
            idx_up = jnp.clip(mb_up, 0, micro_count - 1)
            in_down = jnp.where(is_first, lax.dynamic_index_in_dim(tokens, idx_down, 0, keepdims=False), in_down)
            out_down, kept_down = lax.cond(ok_down, run_down, skip_forward, in_down)
            out_up, kept_up = lax.cond(ok_up, run_up, skip_forward, in_up)
            saved_down = store_inputs(saved_down, kept_down, idx_down, ok_down)
            saved_up = store_inputs(saved_up, kept_up, idx_up, ok_up)
            old_final = lax.dynamic_index_in_dim(finals, idx_up, 0, keepdims=False)
            finals = lax.dynamic_update_index_in_dim(
                finals, jnp.where(ok_up & is_first, out_up, old_final), idx_up, 0)
            recv_down = lax.ppermute(out_down, 'stage', down_perm)
            recv_up = lax.ppermute(out_up, 'stage', up_perm)
            next_up = jnp.where(is_last, out_down, recv_up)
            return (recv_down, next_up, saved_down, saved_up, finals), None

        fwd_init = (zero_act, zero_act, zero_saved, zero_saved, jnp.zeros(tokens.shape, jnp.bfloat16))
        fwd_state, _ = lax.scan(forward_tick, fwd_init, jnp.arange(tick_count))
        saved_down, saved_up, finals = fwd_state[2], fwd_state[3], fwd_state[4]
        error_f32 = finals.astype(jnp.float32) - targets.astype(jnp.float32)
        seed_grads = (error_f32 * (2.0 / (micro_count * tokens_mb))).astype(jnp.bfloat16)
        sse_local = jnp.where(is_first, jnp.sum(error_f32 * error_f32), 0.0)
        loss_value = lax.psum(sse_local, 'stage') / (micro_count * tokens_mb * d_model)

        def run_down_back(operand):
            return segment_backward(operand[1], operand[0], down_weights[0], down_weights[1],
                                    down_weights[2], operand[2])

        def run_up_back(operand):
            return segment_backward(operand[1], operand[0], up_weights[0], up_weights[1],
                                    up_weights[2], operand[2])

        def skip_backward(operand):
            return jnp.zeros_like(operand[0]), operand[2]

        def backward_tick(loop_state, tick_idx):
            grad_up_in, grad_down_in, sums_up, sums_down = loop_state
            mb_up = tick_idx - stage_idx
            mb_down = tick_idx - up_offset
            ok_up = (mb_up >= 0) & (mb_up < micro_count)
            ok_down = (mb_down >= 0) & (mb_down < micro_count)
            idx_up = jnp.clip(mb_up, 0, micro_count - 1)
            idx_down = jnp.clip(mb_down, 0, micro_count - 1)
            grad_up_in = jnp.where(is_first, lax.dynamic_index_in_dim(seed_grads, idx_up, 0, keepdims=False),
                                   grad_up_in)
            kept_up = lax.dynamic_index_in_dim(saved_up, idx_up, 1, keepdims=False)
            kept_down = lax.dynamic_index_in_dim(saved_down, idx_down, 1, keepdims=False)
            grad_up_out, sums_up = lax.cond(ok_up, run_up_back, skip_backward, (grad_up_in, kept_up, sums_up))
            grad_down_out, sums_down = lax.cond(ok_down, run_down_back, skip_backward,
                                                (grad_down_in, kept_down, sums_down))
            recv_up = lax.ppermute(grad_up_out, 'stage', down_perm)
            recv_down = lax.ppermute(grad_down_out, 'stage', up_perm)
            next_down = jnp.where(is_last, grad_up_out, recv_down)
            return (recv_up, next_down, sums_up, sums_down), None

        zero_sums = (jnp.zeros((segment, d_model, d_ff), jnp.float32),
                     jnp.zeros((segment, d_ff, d_model), jnp.float32),
                     jnp.zeros((segment, d_model), jnp.float32))
        back_init = (zero_act, zero_act, zero_sums, zero_sums)
        back_state, _ = lax.scan(backward_tick, back_init, jnp.arange(tick_count))
        sums_up, sums_down = back_state[2], back_state[3]
        grad_w_in = jnp.concatenate([sums_down[0], sums_up[0]], axis=0)
        grad_w_out = jnp.concatenate([sums_down[1], sums_up[1]], axis=0)
        grad_gains = jnp.concatenate([sums_down[2], sums_up[2]], axis=0)
        return grad_w_in, grad_w_out, grad_gains, loss_value.reshape(1)

    block_spec = P(('dp', 'stage'))
    return jax.shard_map(device_step, mesh=mesh,
                         in_specs=(P('dp'), P('dp'), P('stage'), P('stage'), P('stage')),
                         out_specs=(block_spec, block_spec, block_spec, P('dp')),
                         check_vma=False)
```

profile of v0, /device:TPU:0, one launch (start us, length us, event | category | flops | bytes accessed | tf_op | source)
XLA Modules:
  0.0 5915.6 jit_solution(12734641481109568678)
XLA Ops:
  53.2 1738.3 %while.47 = (s32[]{:T(128)}, bf16[1024,1280]{1,0:T(8,128)(2,1)}, bf16[1024,1280]{1,0:T(8,128)(2,1)}, bf16[1,4,1024,1280]{3,2,1,0:T(8,128)(2,1)}, bf16[1,4,1024,1...) while((s32[]{:T(128)}, bf16[1024,1280]{1,0:T(8,128)(2,1)}, ...), condition=%wide.region_7.8_spmd.clone, body=%wide.region_0.7_spmd.clone.sunk | while | flops 53815541760 | bytes 180943504 | solution.py:119
  400.0 60.5 %collective-permute-start = (bf16[1024,1280]{1,0:T(8,128)(2,1)}, bf16[1024,1280]{1,0:T(8,128)(2,1)}, u32[]{:S(2)}, u32[]{:S(2)}) collective-permute-start(bf16[1024,1280]{1,0:T(8,128)(2,1)} %get-tuple-element.944), channel_id=1, source_target_pairs={{0,1},{1,2},{2,3},{3,4},{4,5},{5,6},{6,7}} | collective-permute-start | bytes 7864328 | tf_op jit(solution)/shard_map/while/body/eval_jaxpr/ppermute | solution.py:113
  770.6 64.8 %collective-permute-start = (bf16[1024,1280]{1,0:T(8,128)(2,1)}, bf16[1024,1280]{1,0:T(8,128)(2,1)}, u32[]{:S(2)}, u32[]{:S(2)}) collective-permute-start(bf16[1024,1280]{1,0:T(8,128)(2,1)} %get-tuple-element.944), channel_id=1, source_target_pairs={{0,1},{1,2},{2,3},{3,4},{4,5},{5,6},{6,7}} | collective-permute-start | bytes 7864328 | tf_op jit(solution)/shard_map/while/body/eval_jaxpr/ppermute | solution.py:113
  863.9 59.8 %collective-permute-start = (bf16[1024,1280]{1,0:T(8,128)(2,1)}, bf16[1024,1280]{1,0:T(8,128)(2,1)}, u32[]{:S(2)}, u32[]{:S(2)}) collective-permute-start(bf16[1024,1280]{1,0:T(8,128)(2,1)} %get-tuple-element.944), channel_id=1, source_target_pairs={{0,1},{1,2},{2,3},{3,4},{4,5},{5,6},{6,7}} | collective-permute-start | bytes 7864328 | tf_op jit(solution)/shard_map/while/body/eval_jaxpr/ppermute | solution.py:113
  1013.8 92.7 %collective-permute-start = (bf16[1024,1280]{1,0:T(8,128)(2,1)}, bf16[1024,1280]{1,0:T(8,128)(2,1)}, u32[]{:S(2)}, u32[]{:S(2)}) collective-permute-start(bf16[1024,1280]{1,0:T(8,128)(2,1)} %get-tuple-element.944), channel_id=1, source_target_pairs={{0,1},{1,2},{2,3},{3,4},{4,5},{5,6},{6,7}} | collective-permute-start | bytes 7864328 | tf_op jit(solution)/shard_map/while/body/eval_jaxpr/ppermute | solution.py:113
  1135.0 95.1 %collective-permute-start = (bf16[1024,1280]{1,0:T(8,128)(2,1)}, bf16[1024,1280]{1,0:T(8,128)(2,1)}, u32[]{:S(2)}, u32[]{:S(2)}) collective-permute-start(bf16[1024,1280]{1,0:T(8,128)(2,1)} %get-tuple-element.944), channel_id=1, source_target_pairs={{0,1},{1,2},{2,3},{3,4},{4,5},{5,6},{6,7}} | collective-permute-start | bytes 7864328 | tf_op jit(solution)/shard_map/while/body/eval_jaxpr/ppermute | solution.py:113
  1258.6 74.1 %collective-permute-start = (bf16[1024,1280]{1,0:T(8,128)(2,1)}, bf16[1024,1280]{1,0:T(8,128)(2,1)}, u32[]{:S(2)}, u32[]{:S(2)}) collective-permute-start(bf16[1024,1280]{1,0:T(8,128)(2,1)} %get-tuple-element.944), channel_id=1, source_target_pairs={{0,1},{1,2},{2,3},{3,4},{4,5},{5,6},{6,7}} | collective-permute-start | bytes 7864328 | tf_op jit(solution)/shard_map/while/body/eval_jaxpr/ppermute | solution.py:113
  1878.2 3964.7 %while.48 = (s32[]{:T(128)}, bf16[1024,1280]{1,0:T(8,128)(2,1)}, bf16[1024,1280]{1,0:T(8,128)(2,1)}, f32[1,1280,5120]{2,1,0:T(8,128)}, f32[1,5120,1280]{2,1,0:T(...) while((s32[]{:T(128)}, bf16[1024,1280]{1,0:T(8,128)(2,1)}, ...), condition=%wide.region_19.20_spmd.clone, body=%wide.region_8.19_spmd.clone.sunk | while | flops 134625378304 | bytes 653001536 | solution.py:161
  1896.5 147.4 %conditional.14 = (bf16[1024,1280]{1,0:T(8,128)(2,1)}, f32[1,1280,5120]{2,1,0:T(8,128)}, f32[1,5120,1280]{2,1,0:T(8,128)}, f32[1,1280]{1,0:T(1,128)S(1)}) conditional(s32[]{:T(128)} %convert_element_type.332, (f32[1,1280,5120]{2,1,0:T(8,128)}, f32[1,5120,1280]{2,1,0:T(8,128)}, f32[1,1280]{1,0:T(1,128)S(1)}) %tuple.134, (pred[]{:T(512)}, s32[]{:T(128)}, ...), branch_computations={%region_9.9_spmd, %region_10.13_spmd} | conditional | flops 67310723072 | bytes 301566016 | solution.py:149
  2069.5 147.1 %conditional.14 = (bf16[1024,1280]{1,0:T(8,128)(2,1)}, f32[1,1280,5120]{2,1,0:T(8,128)}, f32[1,5120,1280]{2,1,0:T(8,128)}, f32[1,1280]{1,0:T(1,128)S(1)}) conditional(s32[]{:T(128)} %convert_element_type.332, (f32[1,1280,5120]{2,1,0:T(8,128)}, f32[1,5120,1280]{2,1,0:T(8,128)}, f32[1,1280]{1,0:T(1,128)S(1)}) %tuple.134, (pred[]{:T(512)}, s32[]{:T(128)}, ...), branch_computations={%region_9.9_spmd, %region_10.13_spmd} | conditional | flops 67310723072 | bytes 301566016 | solution.py:149
  2245.0 147.2 %conditional.14 = (bf16[1024,1280]{1,0:T(8,128)(2,1)}, f32[1,1280,5120]{2,1,0:T(8,128)}, f32[1,5120,1280]{2,1,0:T(8,128)}, f32[1,1280]{1,0:T(1,128)S(1)}) conditional(s32[]{:T(128)} %convert_element_type.332, (f32[1,1280,5120]{2,1,0:T(8,128)}, f32[1,5120,1280]{2,1,0:T(8,128)}, f32[1,1280]{1,0:T(1,128)S(1)}) %tuple.134, (pred[]{:T(512)}, s32[]{:T(128)}, ...), branch_computations={%region_9.9_spmd, %region_10.13_spmd} | conditional | flops 67310723072 | bytes 301566016 | solution.py:149
  2444.2 147.4 %conditional.14 = (bf16[1024,1280]{1,0:T(8,128)(2,1)}, f32[1,1280,5120]{2,1,0:T(8,128)}, f32[1,5120,1280]{2,1,0:T(8,128)}, f32[1,1280]{1,0:T(1,128)S(1)}) conditional(s32[]{:T(128)} %convert_element_type.332, (f32[1,1280,5120]{2,1,0:T(8,128)}, f32[1,5120,1280]{2,1,0:T(8,128)}, f32[1,1280]{1,0:T(1,128)S(1)}) %tuple.134, (pred[]{:T(512)}, s32[]{:T(128)}, ...), branch_computations={%region_9.9_spmd, %region_10.13_spmd} | conditional | flops 67310723072 | bytes 301566016 | solution.py:149
  2651.8 170.9 %collective-permute-start.2 = (bf16[1024,1280]{1,0:T(8,128)(2,1)}, bf16[1024,1280]{1,0:T(8,128)(2,1)S(1)}, u32[]{:S(2)}, u32[]{:S(2)}) collective-permute-start(bf16[1024,1280]{1,0:T(8,128)(2,1)} %get-tuple-element.973), channel_id=1, source_target_pairs={{0,1},{1,2},{2,3},{3,4},{4,5},{5,6},{6,7}} | collective-permute-start | bytes 7864328 | tf_op jit(solution)/shard_map/while/body/eval_jaxpr/ppermute | solution.py:152
  2913.7 170.2 %collective-permute-start.2 = (bf16[1024,1280]{1,0:T(8,128)(2,1)}, bf16[1024,1280]{1,0:T(8,128)(2,1)S(1)}, u32[]{:S(2)}, u32[]{:S(2)}) collective-permute-start(bf16[1024,1280]{1,0:T(8,128)(2,1)} %get-tuple-element.973), channel_id=1, source_target_pairs={{0,1},{1,2},{2,3},{3,4},{4,5},{5,6},{6,7}} | collective-permute-start | bytes 7864328 | tf_op jit(solution)/shard_map/while/body/eval_jaxpr/ppermute | solution.py:152
  3170.4 146.4 %collective-permute-start.2 = (bf16[1024,1280]{1,0:T(8,128)(2,1)}, bf16[1024,1280]{1,0:T(8,128)(2,1)S(1)}, u32[]{:S(2)}, u32[]{:S(2)}) collective-permute-start(bf16[1024,1280]{1,0:T(8,128)(2,1)} %get-tuple-element.973), channel_id=1, source_target_pairs={{0,1},{1,2},{2,3},{3,4},{4,5},{5,6},{6,7}} | collective-permute-start | bytes 7864328 | tf_op jit(solution)/shard_map/while/body/eval_jaxpr/ppermute | solution.py:152
  3412.3 176.6 %collective-permute-start.2 = (bf16[1024,1280]{1,0:T(8,128)(2,1)}, bf16[1024,1280]{1,0:T(8,128)(2,1)S(1)}, u32[]{:S(2)}, u32[]{:S(2)}) collective-permute-start(bf16[1024,1280]{1,0:T(8,128)(2,1)} %get-tuple-element.973), channel_id=1, source_target_pairs={{0,1},{1,2},{2,3},{3,4},{4,5},{5,6},{6,7}} | collective-permute-start | bytes 7864328 | tf_op jit(solution)/shard_map/while/body/eval_jaxpr/ppermute | solution.py:152
  3685.4 139.7 %collective-permute-start.2 = (bf16[1024,1280]{1,0:T(8,128)(2,1)}, bf16[1024,1280]{1,0:T(8,128)(2,1)S(1)}, u32[]{:S(2)}, u32[]{:S(2)}) collective-permute-start(bf16[1024,1280]{1,0:T(8,128)(2,1)} %get-tuple-element.973), channel_id=1, source_target_pairs={{0,1},{1,2},{2,3},{3,4},{4,5},{5,6},{6,7}} | collective-permute-start | bytes 7864328 | tf_op jit(solution)/shard_map/while/body/eval_jaxpr/ppermute | solution.py:152
  3913.8 1030.2 %collective-permute-start.2 = (bf16[1024,1280]{1,0:T(8,128)(2,1)}, bf16[1024,1280]{1,0:T(8,128)(2,1)S(1)}, u32[]{:S(2)}, u32[]{:S(2)}) collective-permute-start(bf16[1024,1280]{1,0:T(8,128)(2,1)} %get-tuple-element.973), channel_id=1, source_target_pairs={{0,1},{1,2},{2,3},{3,4},{4,5},{5,6},{6,7}} | collective-permute-start | bytes 7864328 | tf_op jit(solution)/shard_map/while/body/eval_jaxpr/ppermute | solution.py:152
  4952.2 145.5 %conditional.15 = (bf16[1024,1280]{1,0:T(8,128)(2,1)}, f32[1,1280,5120]{2,1,0:T(8,128)}, f32[1,5120,1280]{2,1,0:T(8,128)}, f32[1,1280]{1,0:T(1,128)}) conditional(s32[]{:T(128)} %convert_element_type.333, (f32[1,1280,5120]{2,1,0:T(8,128)}, f32[1,5120,1280]{2,1,0:T(8,128)}, f32[1,1280]{1,0:T(1,128)}) %tuple.112, (s32[]{:T(128)}, ...), branch_computations={%region_14.14_spmd, %region_15.18_spmd.clone} | conditional | flops 67313344512 | bytes 312051872 | solution.py:150
  5144.0 145.7 %conditional.15 = (bf16[1024,1280]{1,0:T(8,128)(2,1)}, f32[1,1280,5120]{2,1,0:T(8,128)}, f32[1,5120,1280]{2,1,0:T(8,128)}, f32[1,1280]{1,0:T(1,128)}) conditional(s32[]{:T(128)} %convert_element_type.333, (f32[1,1280,5120]{2,1,0:T(8,128)}, f32[1,5120,1280]{2,1,0:T(8,128)}, f32[1,1280]{1,0:T(1,128)}) %tuple.112, (s32[]{:T(128)}, ...), branch_computations={%region_14.14_spmd, %region_15.18_spmd.clone} | conditional | flops 67313344512 | bytes 312051872 | solution.py:150
  5298.6 145.3 %collective-permute-start.2 = (bf16[1024,1280]{1,0:T(8,128)(2,1)}, bf16[1024,1280]{1,0:T(8,128)(2,1)S(1)}, u32[]{:S(2)}, u32[]{:S(2)}) collective-permute-start(bf16[1024,1280]{1,0:T(8,128)(2,1)} %get-tuple-element.973), channel_id=1, source_target_pairs={{0,1},{1,2},{2,3},{3,4},{4,5},{5,6},{6,7}} | collective-permute-start | bytes 7864328 | tf_op jit(solution)/shard_map/while/body/eval_jaxpr/ppermute | solution.py:152
  5451.8 145.6 %conditional.15 = (bf16[1024,1280]{1,0:T(8,128)(2,1)}, f32[1,1280,5120]{2,1,0:T(8,128)}, f32[1,5120,1280]{2,1,0:T(8,128)}, f32[1,1280]{1,0:T(1,128)}) conditional(s32[]{:T(128)} %convert_element_type.333, (f32[1,1280,5120]{2,1,0:T(8,128)}, f32[1,5120,1280]{2,1,0:T(8,128)}, f32[1,1280]{1,0:T(1,128)}) %tuple.112, (s32[]{:T(128)}, ...), branch_computations={%region_14.14_spmd, %region_15.18_spmd.clone} | conditional | flops 67313344512 | bytes 312051872 | solution.py:150
  5606.1 65.6 %collective-permute-start.2 = (bf16[1024,1280]{1,0:T(8,128)(2,1)}, bf16[1024,1280]{1,0:T(8,128)(2,1)S(1)}, u32[]{:S(2)}, u32[]{:S(2)}) collective-permute-start(bf16[1024,1280]{1,0:T(8,128)(2,1)} %get-tuple-element.973), channel_id=1, source_target_pairs={{0,1},{1,2},{2,3},{3,4},{4,5},{5,6},{6,7}} | collective-permute-start | bytes 7864328 | tf_op jit(solution)/shard_map/while/body/eval_jaxpr/ppermute | solution.py:152
  5679.9 145.5 %conditional.15 = (bf16[1024,1280]{1,0:T(8,128)(2,1)}, f32[1,1280,5120]{2,1,0:T(8,128)}, f32[1,5120,1280]{2,1,0:T(8,128)}, f32[1,1280]{1,0:T(1,128)}) conditional(s32[]{:T(128)} %convert_element_type.333, (f32[1,1280,5120]{2,1,0:T(8,128)}, f32[1,5120,1280]{2,1,0:T(8,128)}, f32[1,1280]{1,0:T(1,128)}) %tuple.112, (s32[]{:T(128)}, ...), branch_computations={%region_14.14_spmd, %region_15.18_spmd.clone} | conditional | flops 67313344512 | bytes 312051872 | solution.py:150
  (973 shorter events, 3744.0 us)
Async XLA Ops:
  1013.8 115.4 %collective-permute-start = (bf16[1024,1280]{1,0:T(8,128)(2,1)}, bf16[1024,1280]{1,0:T(8,128)(2,1)}, u32[]{:S(2)}, u32[]{:S(2)}) collective-permute-start(bf16[1024,1280]{1,0:T(8,128)(2,1)} %get-tuple-element.944), channel_id=1, source_target_pairs={{0,1},{1,2},{2,3},{3,4},{4,5},{5,6},{6,7}} | collective-permute-start | bytes 7864328 | tf_op jit(solution)/shard_map/while/body/eval_jaxpr/ppermute | solution.py:113
  1135.0 117.8 %collective-permute-start = (bf16[1024,1280]{1,0:T(8,128)(2,1)}, bf16[1024,1280]{1,0:T(8,128)(2,1)}, u32[]{:S(2)}, u32[]{:S(2)}) collective-permute-start(bf16[1024,1280]{1,0:T(8,128)(2,1)} %get-tuple-element.944), channel_id=1, source_target_pairs={{0,1},{1,2},{2,3},{3,4},{4,5},{5,6},{6,7}} | collective-permute-start | bytes 7864328 | tf_op jit(solution)/shard_map/while/body/eval_jaxpr/ppermute | solution.py:113
  1258.6 123.5 %collective-permute-start = (bf16[1024,1280]{1,0:T(8,128)(2,1)}, bf16[1024,1280]{1,0:T(8,128)(2,1)}, u32[]{:S(2)}, u32[]{:S(2)}) collective-permute-start(bf16[1024,1280]{1,0:T(8,128)(2,1)} %get-tuple-element.944), channel_id=1, source_target_pairs={{0,1},{1,2},{2,3},{3,4},{4,5},{5,6},{6,7}} | collective-permute-start | bytes 7864328 | tf_op jit(solution)/shard_map/while/body/eval_jaxpr/ppermute | solution.py:113
  1387.8 93.1 %collective-permute-start = (bf16[1024,1280]{1,0:T(8,128)(2,1)}, bf16[1024,1280]{1,0:T(8,128)(2,1)}, u32[]{:S(2)}, u32[]{:S(2)}) collective-permute-start(bf16[1024,1280]{1,0:T(8,128)(2,1)} %get-tuple-element.944), channel_id=1, source_target_pairs={{0,1},{1,2},{2,3},{3,4},{4,5},{5,6},{6,7}} | collective-permute-start | bytes 7864328 | tf_op jit(solution)/shard_map/while/body/eval_jaxpr/ppermute | solution.py:113
  1578.9 97.8 %collective-permute-start = (bf16[1024,1280]{1,0:T(8,128)(2,1)}, bf16[1024,1280]{1,0:T(8,128)(2,1)}, u32[]{:S(2)}, u32[]{:S(2)}) collective-permute-start(bf16[1024,1280]{1,0:T(8,128)(2,1)} %get-tuple-element.944), channel_id=1, source_target_pairs={{0,1},{1,2},{2,3},{3,4},{4,5},{5,6},{6,7}} | collective-permute-start | bytes 7864328 | tf_op jit(solution)/shard_map/while/body/eval_jaxpr/ppermute | solution.py:113
  1682.5 102.4 %collective-permute-start = (bf16[1024,1280]{1,0:T(8,128)(2,1)}, bf16[1024,1280]{1,0:T(8,128)(2,1)}, u32[]{:S(2)}, u32[]{:S(2)}) collective-permute-start(bf16[1024,1280]{1,0:T(8,128)(2,1)} %get-tuple-element.944), channel_id=1, source_target_pairs={{0,1},{1,2},{2,3},{3,4},{4,5},{5,6},{6,7}} | collective-permute-start | bytes 7864328 | tf_op jit(solution)/shard_map/while/body/eval_jaxpr/ppermute | solution.py:113
  1894.6 150.8 %collective-permute-start.3 = (bf16[1024,1280]{1,0:T(8,128)(2,1)}, bf16[1024,1280]{1,0:T(8,128)(2,1)}, u32[]{:S(2)}, u32[]{:S(2)}) collective-permute-start(bf16[1024,1280]{1,0:T(8,128)(2,1)} %get-tuple-element.974), channel_id=1, source_target_pairs={{1,0},{2,1},{3,2},{4,3},{5,4},{6,5},{7,6}} | collective-permute-start | bytes 7864328 | tf_op jit(solution)/shard_map/while/body/eval_jaxpr/ppermute | solution.py:153
  2067.6 153.2 %collective-permute-start.3 = (bf16[1024,1280]{1,0:T(8,128)(2,1)}, bf16[1024,1280]{1,0:T(8,128)(2,1)}, u32[]{:S(2)}, u32[]{:S(2)}) collective-permute-start(bf16[1024,1280]{1,0:T(8,128)(2,1)} %get-tuple-element.974), channel_id=1, source_target_pairs={{1,0},{2,1},{3,2},{4,3},{5,4},{6,5},{7,6}} | collective-permute-start | bytes 7864328 | tf_op jit(solution)/shard_map/while/body/eval_jaxpr/ppermute | solution.py:153
  2243.1 176.9 %collective-permute-start.3 = (bf16[1024,1280]{1,0:T(8,128)(2,1)}, bf16[1024,1280]{1,0:T(8,128)(2,1)}, u32[]{:S(2)}, u32[]{:S(2)}) collective-permute-start(bf16[1024,1280]{1,0:T(8,128)(2,1)} %get-tuple-element.974), channel_id=1, source_target_pairs={{1,0},{2,1},{3,2},{4,3},{5,4},{6,5},{7,6}} | collective-permute-start | bytes 7864328 | tf_op jit(solution)/shard_map/while/body/eval_jaxpr/ppermute | solution.py:153
  2442.3 178.6 %collective-permute-start.3 = (bf16[1024,1280]{1,0:T(8,128)(2,1)}, bf16[1024,1280]{1,0:T(8,128)(2,1)}, u32[]{:S(2)}, u32[]{:S(2)}) collective-permute-start(bf16[1024,1280]{1,0:T(8,128)(2,1)} %get-tuple-element.974), channel_id=1, source_target_pairs={{1,0},{2,1},{3,2},{4,3},{5,4},{6,5},{7,6}} | collective-permute-start | bytes 7864328 | tf_op jit(solution)/shard_map/while/body/eval_jaxpr/ppermute | solution.py:153
  2643.1 179.6 %collective-permute-start.3 = (bf16[1024,1280]{1,0:T(8,128)(2,1)}, bf16[1024,1280]{1,0:T(8,128)(2,1)}, u32[]{:S(2)}, u32[]{:S(2)}) collective-permute-start(bf16[1024,1280]{1,0:T(8,128)(2,1)} %get-tuple-element.974), channel_id=1, source_target_pairs={{1,0},{2,1},{3,2},{4,3},{5,4},{6,5},{7,6}} | collective-permute-start | bytes 7864328 | tf_op jit(solution)/shard_map/while/body/eval_jaxpr/ppermute | solution.py:153
  2651.8 175.2 %collective-permute-start.2 = (bf16[1024,1280]{1,0:T(8,128)(2,1)}, bf16[1024,1280]{1,0:T(8,128)(2,1)S(1)}, u32[]{:S(2)}, u32[]{:S(2)}) collective-permute-start(bf16[1024,1280]{1,0:T(8,128)(2,1)} %get-tuple-element.973), channel_id=1, source_target_pairs={{0,1},{1,2},{2,3},{3,4},{4,5},{5,6},{6,7}} | collective-permute-start | bytes 7864328 | tf_op jit(solution)/shard_map/while/body/eval_jaxpr/ppermute | solution.py:152
  2904.7 179.2 %collective-permute-start.3 = (bf16[1024,1280]{1,0:T(8,128)(2,1)}, bf16[1024,1280]{1,0:T(8,128)(2,1)}, u32[]{:S(2)}, u32[]{:S(2)}) collective-permute-start(bf16[1024,1280]{1,0:T(8,128)(2,1)} %get-tuple-element.974), channel_id=1, source_target_pairs={{1,0},{2,1},{3,2},{4,3},{5,4},{6,5},{7,6}} | collective-permute-start | bytes 7864328 | tf_op jit(solution)/shard_map/while/body/eval_jaxpr/ppermute | solution.py:153
  2913.7 174.6 %collective-permute-start.2 = (bf16[1024,1280]{1,0:T(8,128)(2,1)}, bf16[1024,1280]{1,0:T(8,128)(2,1)S(1)}, u32[]{:S(2)}, u32[]{:S(2)}) collective-permute-start(bf16[1024,1280]{1,0:T(8,128)(2,1)} %get-tuple-element.973), channel_id=1, source_target_pairs={{0,1},{1,2},{2,3},{3,4},{4,5},{5,6},{6,7}} | collective-permute-start | bytes 7864328 | tf_op jit(solution)/shard_map/while/body/eval_jaxpr/ppermute | solution.py:152
  3165.5 151.3 %collective-permute-start.3 = (bf16[1024,1280]{1,0:T(8,128)(2,1)}, bf16[1024,1280]{1,0:T(8,128)(2,1)}, u32[]{:S(2)}, u32[]{:S(2)}) collective-permute-start(bf16[1024,1280]{1,0:T(8,128)(2,1)} %get-tuple-element.974), channel_id=1, source_target_pairs={{1,0},{2,1},{3,2},{4,3},{5,4},{6,5},{7,6}} | collective-permute-start | bytes 7864328 | tf_op jit(solution)/shard_map/while/body/eval_jaxpr/ppermute | solution.py:153
  3170.4 150.7 %collective-permute-start.2 = (bf16[1024,1280]{1,0:T(8,128)(2,1)}, bf16[1024,1280]{1,0:T(8,128)(2,1)S(1)}, u32[]{:S(2)}, u32[]{:S(2)}) collective-permute-start(bf16[1024,1280]{1,0:T(8,128)(2,1)} %get-tuple-element.973), channel_id=1, source_target_pairs={{0,1},{1,2},{2,3},{3,4},{4,5},{5,6},{6,7}} | collective-permute-start | bytes 7864328 | tf_op jit(solution)/shard_map/while/body/eval_jaxpr/ppermute | solution.py:152
  3403.6 185.3 %collective-permute-start.3 = (bf16[1024,1280]{1,0:T(8,128)(2,1)}, bf16[1024,1280]{1,0:T(8,128)(2,1)}, u32[]{:S(2)}, u32[]{:S(2)}) collective-permute-start(bf16[1024,1280]{1,0:T(8,128)(2,1)} %get-tuple-element.974), channel_id=1, source_target_pairs={{1,0},{2,1},{3,2},{4,3},{5,4},{6,5},{7,6}} | collective-permute-start | bytes 7864328 | tf_op jit(solution)/shard_map/while/body/eval_jaxpr/ppermute | solution.py:153
  3412.3 180.9 %collective-permute-start.2 = (bf16[1024,1280]{1,0:T(8,128)(2,1)}, bf16[1024,1280]{1,0:T(8,128)(2,1)S(1)}, u32[]{:S(2)}, u32[]{:S(2)}) collective-permute-start(bf16[1024,1280]{1,0:T(8,128)(2,1)} %get-tuple-element.973), channel_id=1, source_target_pairs={{0,1},{1,2},{2,3},{3,4},{4,5},{5,6},{6,7}} | collective-permute-start | bytes 7864328 | tf_op jit(solution)/shard_map/while/body/eval_jaxpr/ppermute | solution.py:152
  3676.4 148.7 %collective-permute-start.3 = (bf16[1024,1280]{1,0:T(8,128)(2,1)}, bf16[1024,1280]{1,0:T(8,128)(2,1)}, u32[]{:S(2)}, u32[]{:S(2)}) collective-permute-start(bf16[1024,1280]{1,0:T(8,128)(2,1)} %get-tuple-element.974), channel_id=1, source_target_pairs={{1,0},{2,1},{3,2},{4,3},{5,4},{6,5},{7,6}} | collective-permute-start | bytes 7864328 | tf_op jit(solution)/shard_map/while/body/eval_jaxpr/ppermute | solution.py:153
  3685.4 144.1 %collective-permute-start.2 = (bf16[1024,1280]{1,0:T(8,128)(2,1)}, bf16[1024,1280]{1,0:T(8,128)(2,1)S(1)}, u32[]{:S(2)}, u32[]{:S(2)}) collective-permute-start(bf16[1024,1280]{1,0:T(8,128)(2,1)} %get-tuple-element.973), channel_id=1, source_target_pairs={{0,1},{1,2},{2,3},{3,4},{4,5},{5,6},{6,7}} | collective-permute-start | bytes 7864328 | tf_op jit(solution)/shard_map/while/body/eval_jaxpr/ppermute | solution.py:152
  3908.9 1035.1 %collective-permute-start.3 = (bf16[1024,1280]{1,0:T(8,128)(2,1)}, bf16[1024,1280]{1,0:T(8,128)(2,1)}, u32[]{:S(2)}, u32[]{:S(2)}) collective-permute-start(bf16[1024,1280]{1,0:T(8,128)(2,1)} %get-tuple-element.974), channel_id=1, source_target_pairs={{1,0},{2,1},{3,2},{4,3},{5,4},{6,5},{7,6}} | collective-permute-start | bytes 7864328 | tf_op jit(solution)/shard_map/while/body/eval_jaxpr/ppermute | solution.py:153
  3913.8 1034.5 %collective-permute-start.2 = (bf16[1024,1280]{1,0:T(8,128)(2,1)}, bf16[1024,1280]{1,0:T(8,128)(2,1)S(1)}, u32[]{:S(2)}, u32[]{:S(2)}) collective-permute-start(bf16[1024,1280]{1,0:T(8,128)(2,1)} %get-tuple-element.973), channel_id=1, source_target_pairs={{0,1},{1,2},{2,3},{3,4},{4,5},{5,6},{6,7}} | collective-permute-start | bytes 7864328 | tf_op jit(solution)/shard_map/while/body/eval_jaxpr/ppermute | solution.py:152
  5289.6 154.3 %collective-permute-start.3 = (bf16[1024,1280]{1,0:T(8,128)(2,1)}, bf16[1024,1280]{1,0:T(8,128)(2,1)}, u32[]{:S(2)}, u32[]{:S(2)}) collective-permute-start(bf16[1024,1280]{1,0:T(8,128)(2,1)} %get-tuple-element.974), channel_id=1, source_target_pairs={{1,0},{2,1},{3,2},{4,3},{5,4},{6,5},{7,6}} | collective-permute-start | bytes 7864328 | tf_op jit(solution)/shard_map/while/body/eval_jaxpr/ppermute | solution.py:153
  5298.6 149.7 %collective-permute-start.2 = (bf16[1024,1280]{1,0:T(8,128)(2,1)}, bf16[1024,1280]{1,0:T(8,128)(2,1)S(1)}, u32[]{:S(2)}, u32[]{:S(2)}) collective-permute-start(bf16[1024,1280]{1,0:T(8,128)(2,1)} %get-tuple-element.973), channel_id=1, source_target_pairs={{0,1},{1,2},{2,3},{3,4},{4,5},{5,6},{6,7}} | collective-permute-start | bytes 7864328 | tf_op jit(solution)/shard_map/while/body/eval_jaxpr/ppermute | solution.py:152
  (210 other events, 7589.8 us)
where the time goes:
time: 5950 us; the launch traced here: 5920 us
  starting transfers between devices  3170 us (53%)
  matrix products  1400 us (24%)
  other arithmetic  494 us (8%)
  local copies, waits for them, and re-layouts  424 us (7%)
  loops' own time  338 us (6%)
  waiting for transfers between devices  70.2 us (1%)
    ppermute x19, starting transfers between devices, backward_tick(): recv_up = lax.ppermute(grad_up_out, 'stage', down_perm)  2300 us
    ppermute x19, starting transfers between devices, forward_tick(): recv_down = lax.ppermute(out_down, 'stage', down_perm)  816 us
    dot_general x8, matrix products, layer_forward(): out_f32 = jnp.dot(hidden, second_w, preferred_element_type=jnp.float32)  303 us
    dot_general x8, matrix products, layer_backward(): jnp.einsum('tf,td->fd', hidden, grad_h, preferred_element_type=jnp.float32)  263 us
    dot_general x8, matrix products, layer_backward(): jnp.einsum('td,tf->df', normed, grad_pre, preferred_element_type=jnp.floa...  239 us
    dot_general x8, matrix products, layer_backward(): pre_act = jnp.dot(normed, first_w, preferred_element_type=jnp.float32)  215 us
    dot_general x8, matrix products, layer_backward(): jnp.einsum('td,fd->tf', grad_h, second_w, preferred_element_type=jnp.floa...  202 us
    another operation x19, loops' own time, backward_tick(): lax.cond(ok_down, run_down_back, skip_backward, (grad_down_in, kept_down,...  189 us
  transfers between devices with their start and end apart: 76, of which 21 were waited for; matrix products, arithmetic and copies ran while one was open for 21% of the time, Pallas kernels for 0%

commit v1 on v0

v1 whole, which is shorter than its diff:
```python
import functools

import jax
import jax.numpy as jnp
from jax import lax
from jax.experimental import pallas as pl
from jax.experimental.pallas import tpu as pltpu
from jax.sharding import PartitionSpec as P

BF = jnp.bfloat16
F32 = jnp.float32
EPSILON = 1e-6
CHUNK = 256
HALVES = 2
NT = (((1,), (1,)), ((), ()))
K0 = 0.7978845608028654
K1 = 0.044715
KIND, MB, GOT, PRE, WA, WB, WC, WW = 1, 4, 64, 128, 256, 512, 1024, 2048
ENTRY = 4096


def make_schedule(stages, chunks, t_fwd, t_bwd, lat_same, lat_chip, lat_far):
    dur = (t_fwd, t_fwd, t_bwd, t_bwd)

    def successor(dev, kind):
        if kind in (0, 2):
            return (dev + 1, kind) if dev < stages - 1 else (dev, kind + 1)
        if dev > 0:
            return (dev - 1, kind)
        return (dev, 2) if kind == 1 else None

    def latency(a, b):
        if a == b:
            return 1.0
        low = min(a, b)
        if low % 2 == 0:
            return lat_same
        return lat_far if low % 4 == 3 else lat_chip

    def tail(dev, kind):
        return {0: 4 * stages - dev, 1: 2 * stages + dev, 2: 2 * stages - dev, 3: dev}[kind]

    def simulate(order_key):
        ready = [dict() for _ in range(stages)]
        for m in range(chunks):
            ready[0][(0, m)] = 0.0
        free = [0.0] * stages
        orders = [[] for _ in range(stages)]
        starts = [[] for _ in range(stages)]
        total = 4 * chunks * stages
        done = 0
        while done < total:
            best = None
            for dev in range(stages):
                if ready[dev]:
                    t = max(free[dev], min(ready[dev].values()))
                    if best is None or t < best[0]:
                        best = (t, dev)
            t, dev = best
            cands = [op for op, r in ready[dev].items() if r <= t + 1e-9]
            op = min(cands, key=lambda o: order_key(dev, o[0], o[1]))
            arrive = ready[dev].pop(op)
            orders[dev].append(op)
            starts[dev].append((t, arrive))
            end = t + dur[op[0]]
            free[dev] = end
            nxt = successor(dev, op[0])
            if nxt is not None:
                ready[nxt[0]][(nxt[1], op[1])] = end + latency(dev, nxt[0])
            done += 1
        return max(free), orders, starts

    keys = [
        lambda d, k, m: (-k, m),
        lambda d, k, m: (m - 0.0 * k, -k),
        lambda d, k, m: (m - 2 * k, -k),
        lambda d, k, m: (m - 4 * k, -k),
        lambda d, k, m: (m - 8 * k, -k),
        lambda d, k, m: (-tail(d, k) + m, k),
        lambda d, k, m: (-tail(d, k) + 4 * m, k),
        lambda d, k, m: (-tail(d, k) + 8 * m, k),
        lambda d, k, m: (k, m),
    ]
    results = [simulate(key) for key in keys]
    return min(results, key=lambda r: r[0])


def encode(stages, chunks, orders, starts, margin):
    rows = []
    for dev in range(stages):
        ops = orders[dev]

        def sends(i):
            return 0 <= i < len(ops) and not (dev == 0 and ops[i][0] == 3)

        def local(i):
            return sends(i) and ((dev == stages - 1 and ops[i][0] in (0, 2)) or (dev == 0 and ops[i][0] == 1))

        def feeds(i):
            return local(i) and i + 1 < len(ops) and ops[i + 1] == (ops[i][0] + 1, ops[i][1])

        row = []
        got = False
        seen_top = False
        for i in range(len(ops) + 1):
            e = 0
            if i < len(ops):
                kind, m = ops[i]
                e += KIND * kind + MB * m
                if got:
                    e += GOT
                got = False
                if i + 1 < len(ops):
                    nk, nm = ops[i + 1]
                    t0 = starts[dev][i][0]
                    arrive = starts[dev][i + 1][1]
                    own = dev == 0 and nk == 0
                    dependent = nm == m and nk == kind + 1
                    came_local = (dev == stages - 1 and nk in (1, 3)) or (dev == 0 and nk == 2)
                    prev_local = came_local and ops[i][1] == nm and ops[i][0] == nk - 1
                    if own or (not dependent and not prev_local and arrive + margin <= t0):
                        e += PRE
                        got = True
                if kind in (1, 2) and not seen_top:
                    e += WW
                    seen_top = True
            if feeds(i - 1):
                e += WA
            elif local(i - 1):
                e += WB
            elif i == len(ops) and sends(i - 1):
                e += WB
            if sends(i - 2) and not local(i - 2):
                e += WC
            row.append(e)
        if len(row) % 2:
            row.append(0)
        rows.append([row[j] + ENTRY * row[j + 1] for j in range(0, len(row), 2)])
    return rows


def gelu_and_slope(a):
    a2 = a * a
    t = jnp.tanh(K0 * (a + K1 * (a * a2)))
    cdf = 0.5 * (1.0 + t)
    return a * cdf, cdf + (0.5 * K0) * a * (1.0 - t * t) * (1.0 + (3.0 * K1) * a2)


def pipeline_kernel(stages, table, seed_scale,
                    tokens, targets, w_in, w_out, gains,
                    xs, dhs, ns, us, gs, das, gain_sum, sse_sum,
                    wi, wo, xin, nx, ub, gt, ob,
                    recv_sem, send_sem, in_sem, w_sem, out_sem, g_sem, x_sem):
    me = lax.axis_index('stage')
    chunks = tokens.shape[0] // CHUNK
    d_model = tokens.shape[1]
    d_ff = w_in.shape[2]
    half = d_ff // HALVES
    first = me == 0
    last = me == stages - 1
    n_ops = 4 * chunks

    def weight_copy(row, which):
        src, dst = ((w_in, wi), (w_out, wo))[which]
        return pltpu.make_async_copy(src.at[row], dst.at[row], w_sem.at[2 * row + which])

    weight_copy(0, 0).start()
    weight_copy(0, 1).start()

    barrier = pltpu.get_barrier_semaphore()

    @pl.when(me > 0)
    def _():
        pl.semaphore_signal(barrier, inc=1, device_id={'stage': jnp.maximum(me - 1, 0)})

    @pl.when(me < stages - 1)
    def _():
        pl.semaphore_signal(barrier, inc=1, device_id={'stage': jnp.minimum(me + 1, stages - 1)})

    @pl.when(first | last)
    def _():
        pl.semaphore_wait(barrier, 1)

    @pl.when(jnp.logical_not(first | last))
    def _():
        pl.semaphore_wait(barrier, 2)

    words = []
    for j in range(len(table[0])):
        word = jnp.int32(table[0][j])
        for dev in range(1, stages):
            word = jnp.where(me == dev, jnp.int32(table[dev][j]), word)
        words.append(word)

    def entry(s):
        word = words[0]
        pair = lax.div(s, 2)
        for j in range(1, len(words)):
            word = jnp.where(pair == j, words[j], word)
        return jnp.where(lax.rem(s, 2) == 0, lax.rem(word, ENTRY), lax.div(word, ENTRY))

    def flag(e, bit):
        return lax.rem(lax.div(e, bit), 2) == 1

    def fields(e):
        kind = lax.rem(e, 4)
        m = lax.rem(lax.div(e, MB), chunks)
        row = jnp.where((kind == 1) | (kind == 2), 1, 0)
        return kind, m, row

    def rows_of(m):
        return pl.ds(pl.multiple_of(m * CHUNK, CHUNK), CHUNK)

    def in_copy(slot):
        return pltpu.make_async_copy(tokens.at[pl.ds(0, CHUNK)], xin.at[slot], in_sem.at[slot])

    def start_input(e, slot):
        kind, m, row = fields(e)
        rows = rows_of(m)
        here = (first & ((kind == 0) | (kind == 2))) | (last & ((kind == 1) | (kind == 3)))

        @pl.when(jnp.logical_not(here))
        def _():
            pltpu.make_async_remote_copy(
                src_ref=ob.at[0], dst_ref=xs.at[row, rows], send_sem=send_sem.at[0],
                recv_sem=recv_sem.at[kind * chunks + m], device_id={'stage': me}).wait_recv()

        @pl.when((kind == 0) & first)
        def _():
            pltpu.make_async_copy(tokens.at[rows], xin.at[slot], in_sem.at[slot]).start()

        @pl.when((kind < 2) & jnp.logical_not((kind == 0) & first))
        def _():
            pltpu.make_async_copy(xs.at[row, rows], xin.at[slot], in_sem.at[slot]).start()

        @pl.when(kind >= 2)
        def _():
            pltpu.make_async_copy(dhs.at[row, rows], xin.at[slot], in_sem.at[slot]).start()

    def sent(slot):
        return pltpu.make_async_copy(ob.at[slot], xs.at[0, pl.ds(0, CHUNK)], send_sem.at[slot])

    def slope_copy_in(row, rows, h):
        return pltpu.make_async_copy(gs.at[row, rows, pl.ds(h * half, half)], gt.at[h], g_sem.at[h])

    def start_slopes(e, halves):
        kind, m, row = fields(e)

        @pl.when(kind >= 2)
        def _():
            for h in halves:
                slope_copy_in(row, rows_of(m), h).start()

    def mid_step(s, e, e_next, slot):
        @pl.when(flag(e, WB))
        def _():
            sent(1 - slot).wait()

        @pl.when(flag(e, WC))
        def _():
            sent(slot).wait()

        @pl.when(flag(e, PRE))
        def _():
            start_input(e_next, 1 - slot)

    gain_sum[...] = jnp.zeros_like(gain_sum)
    sse_sum[...] = jnp.zeros_like(sse_sum)
    weight_copy(0, 0).wait()
    weight_copy(0, 1).wait()
    weight_copy(1, 0).start()
    weight_copy(1, 1).start()

    BLK = 64

    def step(s, carry):
        e = entry(s)
        e_next = jnp.where(s + 1 < n_ops, entry(s + 1), 0)
        kind, m, row = fields(e)
        rows = rows_of(m)
        slot = lax.rem(s, 2)

        @pl.when(flag(e, WA))
        def _():
            sent(1 - slot).wait()

        @pl.when(jnp.logical_not(flag(e, GOT)))
        def _():
            start_input(e, slot)

        @pl.when(flag(e, WW))
        def _():
            weight_copy(1, 0).wait()
            weight_copy(1, 1).wait()

        @pl.when(kind < 2)
        def _():
            in_copy(slot).wait()
            gain = gains[row]

            @pl.loop(0, CHUNK // BLK)
            def _(b):
                rb = pl.ds(pl.multiple_of(b * BLK, BLK), BLK)
                x = xin[slot, rb].astype(F32)
                inv = lax.rsqrt(jnp.mean(x * x, axis=-1, keepdims=True) + EPSILON)
                nx[rb] = (x * inv * gain).astype(BF)

            n_copy = pltpu.make_async_copy(nx, ns.at[row, rows], out_sem.at[0])
            n_copy.start()
            g_copies = []
            for h in range(HALVES):
                for j in range(half // 512):
                    lo = h * half + j * 512
                    a = jnp.dot(nx[...], wi[row, :, lo:lo + 512], preferred_element_type=F32)
                    for b in range(CHUNK // 16):
                        u, g = gelu_and_slope(a[b * 16:(b + 1) * 16])
                        ub[b * 16:(b + 1) * 16, lo:lo + 512] = u.astype(BF)
                        gt[h, b * 16:(b + 1) * 16, j * 512:(j + 1) * 512] = g
                g_copy = pltpu.make_async_copy(gt.at[h], gs.at[row, rows, pl.ds(h * half, half)], g_sem.at[h])
                g_copy.start()
                g_copies.append(g_copy)
            u_copy = pltpu.make_async_copy(ub, us.at[row, rows], out_sem.at[1])
            u_copy.start()
            mid_step(s, e, e_next, slot)
            for j in range(d_model // 256):
                cols = slice(j * 256, (j + 1) * 256)
                y = jnp.dot(ub[...], wo[row, :, cols], preferred_element_type=F32)
                ob[slot, :, cols] = (xin[slot, :, cols].astype(F32) + y).astype(BF)
            n_copy.wait()

            @pl.when(first & (kind == 1))
            def _():
                seed_copy = pltpu.make_async_copy(targets.at[rows], nx, x_sem)
                seed_copy.start()
                seed_copy.wait()

                @pl.loop(0, CHUNK // BLK)
                def _(b):
                    rb = pl.ds(pl.multiple_of(b * BLK, BLK), BLK)
                    err = ob[slot, rb].astype(F32) - nx[rb].astype(F32)
                    ob[slot, rb] = (err * seed_scale).astype(BF)
                    sse_sum[...] += jnp.sum((err * err).reshape(BLK // 8, 8, d_model), axis=0)

            u_copy.wait()
            for g_copy in g_copies:
                g_copy.wait()
            send(kind, m, row, rows, slot)
            start_slopes(e_next, (0, 1))

        @pl.when(kind >= 2)
        def _():
            @pl.when((kind == 3) & first)
            def _():
                pltpu.make_async_copy(tokens.at[rows], nx, x_sem).start()

            @pl.when(jnp.logical_not((kind == 3) & first))
            def _():
                pltpu.make_async_copy(xs.at[row, rows], nx, x_sem).start()

            in_copy(slot).wait()
            for h in range(HALVES):
                slope_copy_in(row, rows, h).wait()
                for j in range(half // 512):
                    lo = h * half + j * 512
                    du = lax.dot_general(xin[slot], wo[row, lo:lo + 512, :], NT, preferred_element_type=F32)
                    ub[:, lo:lo + 512] = (du * gt[h, :, j * 512:(j + 1) * 512]).astype(BF)
            da_copy = pltpu.make_async_copy(ub, das.at[row, rows], out_sem.at[1])
            da_copy.start()
            start_slopes(e_next, (0,))
            mid_step(s, e, e_next, slot)
            for j in range(d_model // 256):
                cols = slice(j * 256, (j + 1) * 256)
                gt[1, :, cols] = lax.dot_general(ub[...], wi[row, cols, :], NT, preferred_element_type=F32)
            pltpu.make_async_copy(tokens.at[pl.ds(0, CHUNK)], nx, x_sem).wait()
            gain = gains[row]

            @pl.loop(0, CHUNK // BLK)
            def _(b):
                rb = pl.ds(pl.multiple_of(b * BLK, BLK), BLK)
                x = nx[rb].astype(F32)
                inv = lax.rsqrt(jnp.mean(x * x, axis=-1, keepdims=True) + EPSILON)
                grad_n = gt[1, rb, :d_model]
                q = grad_n * gain
                proj = jnp.mean(q * x, axis=-1, keepdims=True)
                dx = q * inv - x * (inv * inv * inv * proj)
                ob[slot, rb] = (xin[slot, rb].astype(F32) + dx).astype(BF)
                gain_sum[row] += jnp.sum((grad_n * x * inv).reshape(BLK // 8, 8, d_model), axis=0)

            start_slopes(e_next, (1,))
            da_copy.wait()
            send(kind, m, row, rows, slot)

        return carry

    def send(kind, m, row, rows, slot):
        down = (kind == 0) | (kind == 2)
        turn = (last & down) | (first & (kind == 1))
        stop = first & (kind == 3)
        to = jnp.where(down, jnp.minimum(me + 1, stages - 1), jnp.maximum(me - 1, 0))
        remote = jnp.logical_not(turn | stop)

        @pl.when(remote & (kind < 2))
        def _():
            pltpu.make_async_remote_copy(
                src_ref=ob.at[slot], dst_ref=xs.at[row, rows], send_sem=send_sem.at[slot],
                recv_sem=recv_sem.at[kind * chunks + m], device_id={'stage': to}).start()

        @pl.when(remote & (kind >= 2))
        def _():
            pltpu.make_async_remote_copy(
                src_ref=ob.at[slot], dst_ref=dhs.at[row, rows], send_sem=send_sem.at[slot],
                recv_sem=recv_sem.at[kind * chunks + m], device_id={'stage': to}).start()

        @pl.when(turn & (kind == 0))
        def _():
            pltpu.make_async_copy(ob.at[slot], xs.at[1, rows], send_sem.at[slot]).start()

        @pl.when(turn & (kind == 1))
        def _():
            pltpu.make_async_copy(ob.at[slot], dhs.at[1, rows], send_sem.at[slot]).start()

        @pl.when(turn & (kind == 2))
        def _():
            pltpu.make_async_copy(ob.at[slot], dhs.at[0, rows], send_sem.at[slot]).start()

    lax.fori_loop(0, n_ops, step, 0)
    e_end = entry(jnp.int32(n_ops))

    @pl.when(flag(e_end, WB))
    def _():
        sent((n_ops - 1) % 2).wait()

    @pl.when(flag(e_end, WC))
    def _():
        sent(n_ops % 2).wait()


def solution(mesh):
    stages = mesh.shape['stage']

    def device_step(tokens, targets, w_in, w_out, norm_gains):
        micro_count, tokens_mb, d_model = tokens.shape
        d_ff = w_in.shape[2]
        total = micro_count * tokens_mb
        chunks = total // CHUNK
        _, orders, starts = make_schedule(stages, chunks, 8.3, 8.0, 2.5, 9.5, 10.5)
        table = encode(stages, chunks, orders, starts, 2.0)
        any_spec = pl.BlockSpec(memory_space=pl.ANY)
        vmem_spec = pl.BlockSpec(memory_space=pltpu.VMEM)
        shape = jax.ShapeDtypeStruct
        xs, dhs, ns, us, gs, das, gain_sum, sse_sum = pl.pallas_call(
            functools.partial(pipeline_kernel, stages, table, 2.0 / total),
            out_shape=[shape((2, total, d_model), BF), shape((2, total, d_model), BF),
                       shape((2, total, d_model), BF), shape((2, total, d_ff), BF),
                       shape((2, total, d_ff), F32), shape((2, total, d_ff), BF),
                       shape((2, 8, d_model), F32), shape((8, d_model), F32)],
            in_specs=[any_spec] * 4 + [vmem_spec],
            out_specs=[any_spec] * 6 + [vmem_spec] * 2,
            scratch_shapes=[
                pltpu.VMEM((2, d_model, d_ff), BF), pltpu.VMEM((2, d_ff, d_model), BF),
                pltpu.VMEM((2, CHUNK, d_model), BF), pltpu.VMEM((CHUNK, d_model), BF),
                pltpu.VMEM((CHUNK, d_ff), BF), pltpu.VMEM((HALVES, CHUNK, d_ff // HALVES), F32),
                pltpu.VMEM((2, CHUNK, d_model), BF),
                pltpu.SemaphoreType.DMA((4 * chunks,)), pltpu.SemaphoreType.DMA((2,)),
                pltpu.SemaphoreType.DMA((2,)), pltpu.SemaphoreType.DMA((4,)),
                pltpu.SemaphoreType.DMA((2,)), pltpu.SemaphoreType.DMA((HALVES,)),
                pltpu.SemaphoreType.DMA,
            ],
            compiler_params=pltpu.CompilerParams(
                collective_id=0, has_side_effects=True, vmem_limit_bytes=67043328),
            name='vee',
        )(tokens.reshape(total, d_model), targets.reshape(total, d_model), w_in, w_out,
          norm_gains.reshape(2, 1, d_model))
        del xs, gs
        tok = (((1,), (1,)), ((0,), (0,)))
        grad_w_in = lax.dot_general(ns, das, tok, preferred_element_type=F32)
        grad_w_out = lax.dot_general(us, dhs, tok, preferred_element_type=F32)
        grad_gains = jnp.sum(gain_sum, axis=1)
        sse = jnp.where(lax.axis_index('stage') == 0, jnp.sum(sse_sum), 0.0)
        loss_value = lax.psum(sse, 'stage') / (total * d_model)
        return grad_w_in, grad_w_out, grad_gains, loss_value.reshape(1)

    block_spec = P(('dp', 'stage'))
    return jax.shard_map(device_step, mesh=mesh,
                         in_specs=(P('dp'), P('dp'), P('stage'), P('stage'), P('stage')),
                         out_specs=(block_spec, block_spec, block_spec, P('dp')),
                         check_vma=False)
```

time: 5950 us -> 1280 us (0.22)
  starting transfers between devices: 3170 us -> 0 us
  matrix products: 1400 us -> 242 us
  Pallas kernels: 0 us -> 1010 us
  other arithmetic: 494 us -> 1.24 us
  local copies, waits for them, and re-layouts: 424 us -> 1.32 us
  loops' own time: 338 us -> 0 us
  waiting for transfers between devices: 70.2 us -> 0 us
    ppermute x76 -> x0, starting transfers between devices: 3170 us -> none  [the longest x19 2300 us: backward_tick(): recv_up = lax.ppermute(grad_up_out, 'stage', down_perm)]
    dot_general x48 -> x2, matrix products: 1400 us -> 242 us  [the longest x1 121 us: device_step(): grad_w_out = lax.dot_general(us, dhs, tok, preferred_element_type=F32)]
    pallas_call x0 -> x1, Pallas kernels: none -> 1010 us  [device_step(): pl.pallas_call(functools.partial(pipeline_kernel, stages, table, 2.0 / to...]
    another operation x78 -> x0, loops' own time: 338 us -> none  [the longest x19 189 us: backward_tick(): lax.cond(ok_down, run_down_back, skip_backward, (grad_down_in, kept_down,...]
    dynamic_slice x95 -> x0, local copies, waits for them, and re-layouts: 194 us -> none  [the longest x38 107 us: store_inputs(): old_rows = lax.dynamic_index_in_dim(buffer_all, mb_index, 1, keepdims=False)]
    select_n x61 -> x0, other arithmetic: 179 us -> none  [the longest x19 66.6 us: forward_tick(): next_up = jnp.where(is_last, out_down, recv_up)]
    dynamic_update_slice x38 -> x0, other arithmetic: 119 us -> none  [the longest x19 70 us: store_inputs(): lax.dynamic_update_index_in_dim(buffer_all, jnp.where(is_valid, kept_inpu...]
    concatenate x3 -> x0, other arithmetic: 71.2 us -> none  [the longest x1 35.4 us: device_step(): grad_w_in = jnp.concatenate([sums_down[0], sums_up[0]], axis=0)]
  transfers between devices with their start and end apart: 76 -> 0, of which waited for: 21 -> 0; matrix products, arithmetic and copies ran while one was open for 21% -> 0% of each run, Pallas kernels for 0% -> 0%
where the time goes in v1:
time: 1280 us
  Pallas kernels  1010 us (79%)
  matrix products  242 us (19%)
  blocking collectives  22.2 us (2%)
    pallas_call x1, Pallas kernels, device_step(): pl.pallas_call(functools.partial(pipeline_kernel, stages, table, 2.0 / to...  1010 us
    dot_general x1, matrix products, device_step(): grad_w_out = lax.dot_general(us, dhs, tok, preferred_element_type=F32)  121 us
    dot_general x1, matrix products, device_step(): grad_w_in = lax.dot_general(ns, das, tok, preferred_element_type=F32)  121 us

profile of v1, /device:TPU:0, one launch (start us, length us, event | category | flops | bytes accessed | tf_op | source)
XLA Modules:
  0.0 1283.0 jit_solution(837692468419799183)
XLA Ops:
  0.6 1.3 reshape.22.gains
  1.9 1013.6 %vee.1 = (bf16[2,4096,1280]{2,1,0:T(8,128)(2,1)}, bf16[2,4096,1280]{2,1,0:T(8,128)(2,1)}, bf16[2,4096,1280]{2,1,0:T(8,128)(2,1)}, bf16[2,4096,5120]{2,1,0:T(8,12...) custom-call(bf16[4096,1280]{1,0:T(8,128)(2,1)} %bitcast.7, ...), custom_call_target="tpu_custom_call" | custom-call | tf_op jit(solution)/shard_map/vee/pallas_call | solution.py:451
  1015.5 121.0 %fusion.1 = f32[2,5120,1280]{2,1,0:T(8,128)} fusion(bf16[2,4096,5120]{2,1,0:T(8,128)(2,1)} %get-tuple-element.12, bf16[2,4096,1280]{2,1,0:T(8,128)(2,1)} %get-tuple-element.13), kind=kOutput, calls=%fused_computation.1 | convolution fusion | flops 107374182400 | bytes 157286400 | tf_op jit(solution)/shard_map/dot_general | solution.py:477
  1136.5 0.0 copy-start
  1136.5 0.0 copy-start.1
  1136.5 120.6 %fusion = f32[2,1280,5120]{2,1,0:T(8,128)} fusion(bf16[2,4096,1280]{2,1,0:T(8,128)(2,1)} %get-tuple-element.10, bf16[2,4096,5120]{2,1,0:T(8,128)(2,1)} %get-tuple-element.11), kind=kOutput, calls=%fused_computation | convolution fusion | flops 107374182400 | bytes 157286400 | tf_op jit(solution)/shard_map/dot_general | solution.py:476
  1257.1 0.0 copy-done
  1257.1 0.6 reduce_sum.18
  1257.7 0.0 copy-done.1
  1257.7 0.6 reduce_sum.19
  1259.0 22.2 %psum.7 = f32[]{:T(128)} all-reduce(f32[]{:T(128)S(6)} %select_n.4), channel_id=1, replica_groups=mesh['dp'=1,'stage'=8] {'stage'}, use_global_device_ids=true, to_apply=%region_2.3 | all-reduce | flops 1 | bytes 8 | tf_op jit(solution)/shard_map/psum | solution.py:480
Async XLA Ops:
  1136.5 120.6 %copy-start = (f32[2,8,1280]{2,1,0:T(8,128)S(1)}, f32[2,8,1280]{2,1,0:T(8,128)}, u32[]{:S(2)}) copy-start(f32[2,8,1280]{2,1,0:T(8,128)} %get-tuple-element.14) | copy-start | bytes 245764
  1136.5 121.2 %copy-start.1 = (f32[8,1280]{1,0:T(8,128)S(1)}, f32[8,1280]{1,0:T(8,128)}, u32[]{:S(2)}) copy-start(f32[8,1280]{1,0:T(8,128)} %get-tuple-element.15) | copy-start | bytes 122884

commit v2 on v1

--- a/solution.py
+++ b/solution.py
@@ -31,7 +31,7 @@
 
     def latency(a, b):
         if a == b:
-            return 1.0
+            return 2.5
         low = min(a, b)
         if low % 2 == 0:
             return lat_same
@@ -141,16 +141,16 @@
 
 def gelu_and_slope(a):
     a2 = a * a
-    t = jnp.tanh(K0 * (a + K1 * (a * a2)))
-    cdf = 0.5 * (1.0 + t)
-    return a * cdf, cdf + (0.5 * K0) * a * (1.0 - t * t) * (1.0 + (3.0 * K1) * a2)
+    cdf = 0.5 * jnp.tanh(a * (K0 + (K0 * K1) * a2)) + 0.5
+    u = a * cdf
+    return u, cdf + (u * (1.0 - cdf)) * (2.0 * K0 + (6.0 * K0 * K1) * a2)
 
 
 def pipeline_kernel(stages, table, seed_scale,
                     tokens, targets, w_in, w_out, gains,
                     xs, dhs, ns, us, gs, das, gain_sum, sse_sum,
-                    wi, wo, xin, nx, ub, gt, ob,
-                    recv_sem, send_sem, in_sem, w_sem, out_sem, g_sem, x_sem):
+                    wi, wo, xin, nx, ub, gt, ob, sse_acc, sse_in,
+                    recv_sem, send_sem, in_sem, w_sem, out_sem, g_sem, x_sem, sse_send, sse_recv):
     me = lax.axis_index('stage')
     chunks = tokens.shape[0] // CHUNK
     d_model = tokens.shape[1]
@@ -160,12 +160,13 @@
     last = me == stages - 1
     n_ops = 4 * chunks
 
-    def weight_copy(row, which):
-        src, dst = ((w_in, wi), (w_out, wo))[which]
-        return pltpu.make_async_copy(src.at[row], dst.at[row], w_sem.at[2 * row + which])
-
-    weight_copy(0, 0).start()
-    weight_copy(0, 1).start()
+    def weight_copies(row):
+        copies = [pltpu.make_async_copy(w_in.at[row, :, pl.ds(h * half, half)], wi.at[row, h],
+                                        w_sem.at[3 * row + h]) for h in range(HALVES)]
+        return copies + [pltpu.make_async_copy(w_out.at[row], wo.at[row], w_sem.at[3 * row + HALVES])]
+
+    for copy in weight_copies(0):
+        copy.start()
 
     barrier = pltpu.get_barrier_semaphore()
 
@@ -177,7 +178,15 @@
     def _():
         pl.semaphore_signal(barrier, inc=1, device_id={'stage': jnp.minimum(me + 1, stages - 1)})
 
-    @pl.when(first | last)
+    @pl.when(me > 1)
+    def _():
+        pl.semaphore_signal(barrier, inc=1, device_id={'stage': 0})
+
+    @pl.when(first)
+    def _():
+        pl.semaphore_wait(barrier, stages - 1)
+
+    @pl.when(last)
     def _():
         pl.semaphore_wait(barrier, 1)
 
@@ -265,11 +274,16 @@
             start_input(e_next, 1 - slot)
 
     gain_sum[...] = jnp.zeros_like(gain_sum)
-    sse_sum[...] = jnp.zeros_like(sse_sum)
-    weight_copy(0, 0).wait()
-    weight_copy(0, 1).wait()
-    weight_copy(1, 0).start()
-    weight_copy(1, 1).start()
+    sse_acc[...] = jnp.zeros_like(sse_acc)
+    for copy in weight_copies(0):
+        copy.wait()
+    for copy in weight_copies(1):
+        copy.start()
+
+    def sse_copy(dev):
+        return pltpu.make_async_remote_copy(
+            src_ref=sse_sum, dst_ref=sse_in, send_sem=sse_send.at[dev], recv_sem=sse_recv,
+            device_id={'stage': dev})
 
     BLK = 64
 
@@ -290,8 +304,8 @@
 
         @pl.when(flag(e, WW))
         def _():
-            weight_copy(1, 0).wait()
-            weight_copy(1, 1).wait()
+            for copy in weight_copies(1):
+                copy.wait()
 
         @pl.when(kind < 2)
         def _():
@@ -308,24 +322,35 @@
             n_copy = pltpu.make_async_copy(nx, ns.at[row, rows], out_sem.at[0])
             n_copy.start()
             g_copies = []
+            u_copies = []
             for h in range(HALVES):
                 for j in range(half // 512):
-                    lo = h * half + j * 512
-                    a = jnp.dot(nx[...], wi[row, :, lo:lo + 512], preferred_element_type=F32)
+                    a = jnp.dot(nx[...], wi[row, h, :, j * 512:(j + 1) * 512], preferred_element_type=F32)
                     for b in range(CHUNK // 16):
                         u, g = gelu_and_slope(a[b * 16:(b + 1) * 16])
-                        ub[b * 16:(b + 1) * 16, lo:lo + 512] = u.astype(BF)
+                        ub[h, b * 16:(b + 1) * 16, j * 512:(j + 1) * 512] = u.astype(BF)
                         gt[h, b * 16:(b + 1) * 16, j * 512:(j + 1) * 512] = g
                 g_copy = pltpu.make_async_copy(gt.at[h], gs.at[row, rows, pl.ds(h * half, half)], g_sem.at[h])
                 g_copy.start()
                 g_copies.append(g_copy)
-            u_copy = pltpu.make_async_copy(ub, us.at[row, rows], out_sem.at[1])
-            u_copy.start()
+                u_copy = pltpu.make_async_copy(ub.at[h], us.at[row, rows, pl.ds(h * half, half)],
+                                               out_sem.at[1 + h])
+                u_copy.start()
+                u_copies.append(u_copy)
             mid_step(s, e, e_next, slot)
-            for j in range(d_model // 256):
-                cols = slice(j * 256, (j + 1) * 256)
-                y = jnp.dot(ub[...], wo[row, :, cols], preferred_element_type=F32)
-                ob[slot, :, cols] = (xin[slot, :, cols].astype(F32) + y).astype(BF)
+
+            def second(rb, cols):
+                y = jnp.dot(ub[0, rb, :], wo[row, :half, cols], preferred_element_type=F32)
+                y += jnp.dot(ub[1, rb, :], wo[row, half:, cols], preferred_element_type=F32)
+                ob[slot, rb, cols] = (xin[slot, rb, cols].astype(F32) + y).astype(BF)
+
+            for j in range(d_model // 256 - 1):
+                second(slice(0, CHUNK), slice(j * 256, (j + 1) * 256))
+            for g_copy in g_copies:
+                g_copy.wait()
+            start_slopes(e_next, (0, 1))
+            second(slice(0, CHUNK // 2), slice(d_model - 256, d_model))
+            second(slice(CHUNK // 2, CHUNK), slice(d_model - 256, d_model))
             n_copy.wait()
 
             @pl.when(first & (kind == 1))
@@ -339,13 +364,23 @@
                     rb = pl.ds(pl.multiple_of(b * BLK, BLK), BLK)
                     err = ob[slot, rb].astype(F32) - nx[rb].astype(F32)
                     ob[slot, rb] = (err * seed_scale).astype(BF)
-                    sse_sum[...] += jnp.sum((err * err).reshape(BLK // 8, 8, d_model), axis=0)
-
-            u_copy.wait()
-            for g_copy in g_copies:
-                g_copy.wait()
+                    sse_acc[...] += jnp.sum((err * err).reshape(BLK // 8, 8, d_model), axis=0)
+
+                @pl.when(m == chunks - 1)
+                def _():
+                    acc = sse_acc[:, :128]
+                    for j in range(1, d_model // 128):
+                        acc += sse_acc[:, j * 128:(j + 1) * 128]
+                    sse_sum[...] = acc
+
+            for u_copy in u_copies:
+                u_copy.wait()
             send(kind, m, row, rows, slot)
-            start_slopes(e_next, (0, 1))
+
+            @pl.when(first & (kind == 1) & (m == chunks - 1))
+            def _():
+                for dev in range(1, stages):
+                    sse_copy(dev).start()
 
         @pl.when(kind >= 2)
         def _():
@@ -363,14 +398,22 @@
                 for j in range(half // 512):
                     lo = h * half + j * 512
                     du = lax.dot_general(xin[slot], wo[row, lo:lo + 512, :], NT, preferred_element_type=F32)
-                    ub[:, lo:lo + 512] = (du * gt[h, :, j * 512:(j + 1) * 512]).astype(BF)
-            da_copy = pltpu.make_async_copy(ub, das.at[row, rows], out_sem.at[1])
-            da_copy.start()
+                    ub[h, :, j * 512:(j + 1) * 512] = (du * gt[h, :, j * 512:(j + 1) * 512]).astype(BF)
+            da_copies = [pltpu.make_async_copy(ub.at[h], das.at[row, rows, pl.ds(h * half, half)],
+                                               out_sem.at[1 + h]) for h in range(HALVES)]
+            for da_copy in da_copies:
+                da_copy.start()
             start_slopes(e_next, (0,))
             mid_step(s, e, e_next, slot)
-            for j in range(d_model // 256):
+            for j in range(d_model // 256 - 1):
                 cols = slice(j * 256, (j + 1) * 256)
-                gt[1, :, cols] = lax.dot_general(ub[...], wi[row, cols, :], NT, preferred_element_type=F32)
+                gt[1, :, cols] = (
+                    lax.dot_general(ub[0], wi[row, 0, cols, :], NT, preferred_element_type=F32)
+                    + lax.dot_general(ub[1], wi[row, 1, cols, :], NT, preferred_element_type=F32))
+            for h in range(HALVES):
+                gt[1, :, d_model + (h - 1) * 256:d_model + h * 256] = lax.dot_general(
+                    ub[h], wi[row, h, d_model - 256:, :], NT, preferred_element_type=F32)
+            gt[1, :, d_model - 256:d_model] += gt[1, :, d_model:d_model + 256]
             pltpu.make_async_copy(tokens.at[pl.ds(0, CHUNK)], nx, x_sem).wait()
             gain = gains[row]
 
@@ -387,7 +430,8 @@
                 gain_sum[row] += jnp.sum((grad_n * x * inv).reshape(BLK // 8, 8, d_model), axis=0)
 
             start_slopes(e_next, (1,))
-            da_copy.wait()
+            for da_copy in da_copies:
+                da_copy.wait()
             send(kind, m, row, rows, slot)
 
         return carry
@@ -434,6 +478,16 @@
     def _():
         sent(n_ops % 2).wait()
 
+    @pl.when(first)
+    def _():
+        for dev in range(1, stages):
+            sse_copy(dev).wait_send()
+
+    @pl.when(jnp.logical_not(first))
+    def _():
+        sse_copy(0).wait_recv()
+        sse_sum[...] = sse_in[...]
+
 
 def solution(mesh):
     stages = mesh.shape['stage']
@@ -443,7 +497,7 @@
         d_ff = w_in.shape[2]
         total = micro_count * tokens_mb
         chunks = total // CHUNK
-        _, orders, starts = make_schedule(stages, chunks, 8.3, 8.0, 2.5, 9.5, 10.5)
+        _, orders, starts = make_schedule(stages, chunks, 10.5, 9.5, 2.7, 9.5, 10.5)
         table = encode(stages, chunks, orders, starts, 2.0)
         any_spec = pl.BlockSpec(memory_space=pl.ANY)
         vmem_spec = pl.BlockSpec(memory_space=pltpu.VMEM)
@@ -453,18 +507,19 @@
             out_shape=[shape((2, total, d_model), BF), shape((2, total, d_model), BF),
                        shape((2, total, d_model), BF), shape((2, total, d_ff), BF),
                        shape((2, total, d_ff), F32), shape((2, total, d_ff), BF),
-                       shape((2, 8, d_model), F32), shape((8, d_model), F32)],
+                       shape((2, 8, d_model), F32), shape((8, 128), F32)],
             in_specs=[any_spec] * 4 + [vmem_spec],
             out_specs=[any_spec] * 6 + [vmem_spec] * 2,
             scratch_shapes=[
-                pltpu.VMEM((2, d_model, d_ff), BF), pltpu.VMEM((2, d_ff, d_model), BF),
+                pltpu.VMEM((2, HALVES, d_model, d_ff // HALVES), BF), pltpu.VMEM((2, d_ff, d_model), BF),
                 pltpu.VMEM((2, CHUNK, d_model), BF), pltpu.VMEM((CHUNK, d_model), BF),
-                pltpu.VMEM((CHUNK, d_ff), BF), pltpu.VMEM((HALVES, CHUNK, d_ff // HALVES), F32),
-                pltpu.VMEM((2, CHUNK, d_model), BF),
+                pltpu.VMEM((HALVES, CHUNK, d_ff // HALVES), BF), pltpu.VMEM((HALVES, CHUNK, d_ff // HALVES), F32),
+                pltpu.VMEM((2, CHUNK, d_model), BF), pltpu.VMEM((8, d_model), F32),
+                pltpu.VMEM((8, 128), F32),
                 pltpu.SemaphoreType.DMA((4 * chunks,)), pltpu.SemaphoreType.DMA((2,)),
-                pltpu.SemaphoreType.DMA((2,)), pltpu.SemaphoreType.DMA((4,)),
-                pltpu.SemaphoreType.DMA((2,)), pltpu.SemaphoreType.DMA((HALVES,)),
-                pltpu.SemaphoreType.DMA,
+                pltpu.SemaphoreType.DMA((2,)), pltpu.SemaphoreType.DMA((2 * HALVES + 2,)),
+                pltpu.SemaphoreType.DMA((HALVES + 1,)), pltpu.SemaphoreType.DMA((HALVES,)),
+                pltpu.SemaphoreType.DMA, pltpu.SemaphoreType.DMA((stages,)), pltpu.SemaphoreType.DMA,
             ],
             compiler_params=pltpu.CompilerParams(
                 collective_id=0, has_side_effects=True, vmem_limit_bytes=67043328),
@@ -476,8 +531,7 @@
         grad_w_in = lax.dot_general(ns, das, tok, preferred_element_type=F32)
         grad_w_out = lax.dot_general(us, dhs, tok, preferred_element_type=F32)
         grad_gains = jnp.sum(gain_sum, axis=1)
-        sse = jnp.where(lax.axis_index('stage') == 0, jnp.sum(sse_sum), 0.0)
-        loss_value = lax.psum(sse, 'stage') / (total * d_model)
+        loss_value = jnp.sum(sse_sum) / (total * d_model)
         return grad_w_in, grad_w_out, grad_gains, loss_value.reshape(1)
 
     block_spec = P(('dp', 'stage'))

time: 1280 us -> 1160 us (0.906)
  Pallas kernels: 1010 us -> 910 us
  blocking collectives: 22.2 us -> 0 us
    pallas_call x1, Pallas kernels: 1010 us -> 910 us  [device_step(): pl.pallas_call(functools.partial(pipeline_kernel, stages, table, 2.0 / to...]
    psum x1 -> x0, blocking collectives: 22.2 us -> none  [device_step(): loss_value = lax.psum(sse, 'stage') / (total * d_model)]
where the time goes in v2:
time: 1160 us
  Pallas kernels  910 us (78%)
  matrix products  241 us (21%)
    pallas_call x1, Pallas kernels, device_step(): pl.pallas_call(functools.partial(pipeline_kernel, stages, table, 2.0 / to...  910 us
    dot_general x1, matrix products, device_step(): grad_w_out = lax.dot_general(us, dhs, tok, preferred_element_type=F32)  121 us
    dot_general x1, matrix products, device_step(): grad_w_in = lax.dot_general(ns, das, tok, preferred_element_type=F32)  120 us

profile of v2, /device:TPU:0, one launch (start us, length us, event | category | flops | bytes accessed | tf_op | source)
XLA Modules:
  0.0 1157.4 jit_solution(3749019374278172165)
XLA Ops:
  0.6 1.3 reshape.22.gains
  1.9 910.4 %vee.1 = (bf16[2,4096,1280]{2,1,0:T(8,128)(2,1)}, bf16[2,4096,1280]{2,1,0:T(8,128)(2,1)}, bf16[2,4096,1280]{2,1,0:T(8,128)(2,1)}, bf16[2,4096,5120]{2,1,0:T(8,12...) custom-call(bf16[4096,1280]{1,0:T(8,128)(2,1)} %bitcast.7, ...), custom_call_target="tpu_custom_call" | custom-call | tf_op jit(solution)/shard_map/vee/pallas_call | solution.py:505
  912.3 1.3 reduce_sum.19
  914.2 0.0 copy-start
  914.3 120.4 %fusion = f32[2,1280,5120]{2,1,0:T(8,128)} fusion(bf16[2,4096,1280]{2,1,0:T(8,128)(2,1)} %get-tuple-element.10, bf16[2,4096,5120]{2,1,0:T(8,128)(2,1)} %get-tuple-element.11), kind=kOutput, calls=%fused_computation | convolution fusion | flops 107374182400 | bytes 157286400 | tf_op jit(solution)/shard_map/dot_general | solution.py:531
  1034.6 0.0 copy-done
  1034.6 0.6 reduce_sum.18
  1035.3 121.0 %fusion.1 = f32[2,5120,1280]{2,1,0:T(8,128)} fusion(bf16[2,4096,5120]{2,1,0:T(8,128)(2,1)} %get-tuple-element.12, bf16[2,4096,1280]{2,1,0:T(8,128)(2,1)} %get-tuple-element.13), kind=kOutput, calls=%fused_computation.1 | convolution fusion | flops 107374182400 | bytes 157286400 | tf_op jit(solution)/shard_map/dot_general | solution.py:532
Async XLA Ops:
  914.2 120.4 %copy-start = (f32[2,8,1280]{2,1,0:T(8,128)S(1)}, f32[2,8,1280]{2,1,0:T(8,128)}, u32[]{:S(2)}) copy-start(f32[2,8,1280]{2,1,0:T(8,128)} %get-tuple-element.14) | copy-start | bytes 245764

commit v3 on v2

--- a/solution.py
+++ b/solution.py
@@ -11,6 +11,7 @@
 F32 = jnp.float32
 EPSILON = 1e-6
 CHUNK = 256
+SUB = 128
 HALVES = 2
 NT = (((1,), (1,)), ((), ()))
 K0 = 0.7978845608028654
@@ -66,7 +67,10 @@
             free[dev] = end
             nxt = successor(dev, op[0])
             if nxt is not None:
-                ready[nxt[0]][(nxt[1], op[1])] = end + latency(dev, nxt[0])
+                wait = latency(dev, nxt[0])
+                if op[0] < 2 and dev != nxt[0]:
+                    wait = 0.5 * (wait + 1.5) - 0.5 * t_fwd
+                ready[nxt[0]][(nxt[1], op[1])] = end + wait
             done += 1
         return max(free), orders, starts
 
@@ -118,7 +122,7 @@
                     dependent = nm == m and nk == kind + 1
                     came_local = (dev == stages - 1 and nk in (1, 3)) or (dev == 0 and nk == 2)
                     prev_local = came_local and ops[i][1] == nm and ops[i][0] == nk - 1
-                    if own or (not dependent and not prev_local and arrive + margin <= t0):
+                    if own or (not dependent and not prev_local and arrive + margin + (6.0 if nk < 2 else 0.0) <= t0):
                         e += PRE
                         got = True
                 if kind in (1, 2) and not seen_top:
@@ -149,8 +153,8 @@
 def pipeline_kernel(stages, table, seed_scale,
                     tokens, targets, w_in, w_out, gains,
                     xs, dhs, ns, us, gs, das, gain_sum, sse_sum,
-                    wi, wo, xin, nx, ub, gt, ob, sse_acc, sse_in,
-                    recv_sem, send_sem, in_sem, w_sem, out_sem, g_sem, x_sem, sse_send, sse_recv):
+                    wi, wo, xin, nx, ub, gt, ob, yt, sse_acc, sse_in,
+                    recv_sem, half_sem, send_sem, in_sem, w_sem, out_sem, g_sem, x_sem, sse_send, sse_recv):
     me = lax.axis_index('stage')
     chunks = tokens.shape[0] // CHUNK
     d_model = tokens.shape[1]
@@ -223,15 +227,47 @@
     def in_copy(slot):
         return pltpu.make_async_copy(tokens.at[pl.ds(0, CHUNK)], xin.at[slot], in_sem.at[slot])
 
+    def sub_rows(m, sub):
+        return pl.ds(pl.multiple_of(m * CHUNK + sub * SUB, SUB), SUB)
+
+    def arrival(kind, m, row, sub):
+        return pltpu.make_async_remote_copy(
+            src_ref=ob.at[0, pl.ds(0, SUB)], dst_ref=xs.at[row, sub_rows(m, sub)], send_sem=send_sem.at[0],
+            recv_sem=half_sem.at[(kind * chunks + m) * 2 + sub], device_id={'stage': me})
+
+    def start_half(kind, m, row, slot, sub):
+        from_tokens = (kind == 0) & first
+        here = from_tokens | (last & (kind == 1))
+        part = pl.ds(pl.multiple_of(sub * SUB, SUB), SUB)
+
+        @pl.when(jnp.logical_not(here))
+        def _():
+            arrival(kind, m, row, sub).wait_recv()
+
+        @pl.when(from_tokens)
+        def _():
+            pltpu.make_async_copy(tokens.at[sub_rows(m, sub)], xin.at[slot, part], in_sem.at[slot]).start()
+
+        @pl.when(jnp.logical_not(from_tokens))
+        def _():
+            pltpu.make_async_copy(xs.at[row, sub_rows(m, sub)], xin.at[slot, part], in_sem.at[slot]).start()
+
+        pltpu.make_async_copy(tokens.at[pl.ds(0, SUB)], xin.at[slot, part], in_sem.at[slot]).wait()
+
     def start_input(e, slot):
         kind, m, row = fields(e)
         rows = rows_of(m)
         here = (first & ((kind == 0) | (kind == 2))) | (last & ((kind == 1) | (kind == 3)))
 
-        @pl.when(jnp.logical_not(here))
+        @pl.when(jnp.logical_not(here) & (kind < 2))
+        def _():
+            for sub in range(2):
+                arrival(kind, m, row, sub).wait_recv()
+
+        @pl.when(jnp.logical_not(here) & (kind >= 2))
         def _():
             pltpu.make_async_remote_copy(
-                src_ref=ob.at[0], dst_ref=xs.at[row, rows], send_sem=send_sem.at[0],
+                src_ref=ob.at[0], dst_ref=dhs.at[row, rows], send_sem=send_sem.at[0],
                 recv_sem=recv_sem.at[kind * chunks + m], device_id={'stage': me}).wait_recv()
 
         @pl.when((kind == 0) & first)
@@ -260,25 +296,23 @@
             for h in halves:
                 slope_copy_in(row, rows_of(m), h).start()
 
-    def mid_step(s, e, e_next, slot):
-        @pl.when(flag(e, WB))
+    def mid_step(e, e_next, slot, begin, end):
+        @pl.when(begin & flag(e, WB))
         def _():
             sent(1 - slot).wait()
 
-        @pl.when(flag(e, WC))
+        @pl.when(begin & flag(e, WC))
         def _():
             sent(slot).wait()
 
-        @pl.when(flag(e, PRE))
+        @pl.when(end & flag(e, PRE))
         def _():
             start_input(e_next, 1 - slot)
 
     gain_sum[...] = jnp.zeros_like(gain_sum)
     sse_acc[...] = jnp.zeros_like(sse_acc)
-    for copy in weight_copies(0):
+    for copy in weight_copies(0)[:HALVES]:
         copy.wait()
-    for copy in weight_copies(1):
-        copy.start()
 
     def sse_copy(dev):
         return pltpu.make_async_remote_copy(
@@ -298,7 +332,7 @@
         def _():
             sent(1 - slot).wait()
 
-        @pl.when(jnp.logical_not(flag(e, GOT)))
+        @pl.when(jnp.logical_not(flag(e, GOT)) & (kind >= 2))
         def _():
             start_input(e, slot)
 
@@ -309,76 +343,97 @@
 
         @pl.when(kind < 2)
         def _():
-            in_copy(slot).wait()
+            @pl.when(flag(e, GOT))
+            def _():
+                in_copy(slot).wait()
+
             gain = gains[row]
-
-            @pl.loop(0, CHUNK // BLK)
-            def _(b):
-                rb = pl.ds(pl.multiple_of(b * BLK, BLK), BLK)
-                x = xin[slot, rb].astype(F32)
-                inv = lax.rsqrt(jnp.mean(x * x, axis=-1, keepdims=True) + EPSILON)
-                nx[rb] = (x * inv * gain).astype(BF)
-
             n_copy = pltpu.make_async_copy(nx, ns.at[row, rows], out_sem.at[0])
-            n_copy.start()
-            g_copies = []
-            u_copies = []
-            for h in range(HALVES):
-                for j in range(half // 512):
-                    a = jnp.dot(nx[...], wi[row, h, :, j * 512:(j + 1) * 512], preferred_element_type=F32)
-                    for b in range(CHUNK // 16):
-                        u, g = gelu_and_slope(a[b * 16:(b + 1) * 16])
-                        ub[h, b * 16:(b + 1) * 16, j * 512:(j + 1) * 512] = u.astype(BF)
-                        gt[h, b * 16:(b + 1) * 16, j * 512:(j + 1) * 512] = g
-                g_copy = pltpu.make_async_copy(gt.at[h], gs.at[row, rows, pl.ds(h * half, half)], g_sem.at[h])
-                g_copy.start()
-                g_copies.append(g_copy)
-                u_copy = pltpu.make_async_copy(ub.at[h], us.at[row, rows, pl.ds(h * half, half)],
-                                               out_sem.at[1 + h])
-                u_copy.start()
-                u_copies.append(u_copy)
-            mid_step(s, e, e_next, slot)
-
-            def second(rb, cols):
-                y = jnp.dot(ub[0, rb, :], wo[row, :half, cols], preferred_element_type=F32)
-                y += jnp.dot(ub[1, rb, :], wo[row, half:, cols], preferred_element_type=F32)
-                ob[slot, rb, cols] = (xin[slot, rb, cols].astype(F32) + y).astype(BF)
-
-            for j in range(d_model // 256 - 1):
-                second(slice(0, CHUNK), slice(j * 256, (j + 1) * 256))
+            g_copies = [pltpu.make_async_copy(gt.at[h], gs.at[row, rows, pl.ds(h * half, half)], g_sem.at[h])
+                        for h in range(HALVES)]
+            u_copies = [pltpu.make_async_copy(ub.at[h], us.at[row, rows, pl.ds(h * half, half)],
+                                              out_sem.at[1 + h]) for h in range(HALVES)]
+
+            @pl.loop(0, CHUNK // SUB)
+            def _(sub):
+                base = pl.multiple_of(sub * SUB, SUB)
+                part = pl.ds(base, SUB)
+                place = sub_rows(m, sub)
+
+                @pl.when(jnp.logical_not(flag(e, GOT)))
+                def _():
+                    start_half(kind, m, row, slot, sub)
+
+                @pl.loop(0, SUB // BLK)
+                def _(b):
+                    rb = pl.ds(pl.multiple_of(base + b * BLK, BLK), BLK)
+                    x = xin[slot, rb].astype(F32)
+                    inv = lax.rsqrt(jnp.mean(x * x, axis=-1, keepdims=True) + EPSILON)
+                    nx[rb] = (x * inv * gain).astype(BF)
+
+                pltpu.make_async_copy(nx.at[part], ns.at[row, place], out_sem.at[0]).start()
+                for h in range(HALVES):
+                    for j in range(half // 512):
+                        a = jnp.dot(nx[part], wi[row, h, :, j * 512:(j + 1) * 512], preferred_element_type=F32)
+                        for b in range(SUB // 16):
+                            u, g = gelu_and_slope(a[b * 16:(b + 1) * 16])
+                            rb = pl.ds(pl.multiple_of(base + b * 16, 16), 16)
+                            ub[h, rb, j * 512:(j + 1) * 512] = u.astype(BF)
+                            gt[h, rb, j * 512:(j + 1) * 512] = g
+                    pltpu.make_async_copy(gt.at[h, part], gs.at[row, place, pl.ds(h * half, half)],
+                                          g_sem.at[h]).start()
+                    pltpu.make_async_copy(ub.at[h, part], us.at[row, place, pl.ds(h * half, half)],
+                                          out_sem.at[1 + h]).start()
+
+                @pl.when((s == 0) & (sub == 0))
+                def _():
+                    weight_copies(0)[HALVES].wait()
+                    for copy in weight_copies(1):
+                        copy.start()
+
+                mid_step(e, e_next, slot, sub == 0, sub == 1)
+                for j in range(d_model // 256 - 1):
+                    cols = slice(j * 256, (j + 1) * 256)
+                    y = jnp.dot(ub[0, part, :], wo[row, :half, cols], preferred_element_type=F32)
+                    y += jnp.dot(ub[1, part, :], wo[row, half:, cols], preferred_element_type=F32)
+                    ob[slot, part, cols] = (xin[slot, part, cols].astype(F32) + y).astype(BF)
+                cols = slice(d_model - 256, d_model)
+                yt[0] = jnp.dot(ub[0, part, :], wo[row, :half, cols], preferred_element_type=F32)
+                yt[1] = jnp.dot(ub[1, part, :], wo[row, half:, cols], preferred_element_type=F32)
+                ob[slot, part, cols] = (xin[slot, part, cols].astype(F32) + (yt[0] + yt[1])).astype(BF)
+
+                @pl.when(first & (kind == 1))
+                def _():
+                    pltpu.make_async_copy(nx.at[part], ns.at[row, place], out_sem.at[0]).wait()
+                    seed_copy = pltpu.make_async_copy(targets.at[place], nx.at[part], x_sem)
+                    seed_copy.start()
+                    seed_copy.wait()
+
+                    @pl.loop(0, SUB // BLK)
+                    def _(b):
+                        rb = pl.ds(pl.multiple_of(base + b * BLK, BLK), BLK)
+                        err = ob[slot, rb].astype(F32) - nx[rb].astype(F32)
+                        ob[slot, rb] = (err * seed_scale).astype(BF)
+                        sse_acc[...] += jnp.sum((err * err).reshape(BLK // 8, 8, d_model), axis=0)
+
+                send_half(kind, m, row, slot, sub)
+
+            @pl.when(jnp.logical_not(first & (kind == 1)))
+            def _():
+                n_copy.wait()
+
             for g_copy in g_copies:
                 g_copy.wait()
             start_slopes(e_next, (0, 1))
-            second(slice(0, CHUNK // 2), slice(d_model - 256, d_model))
-            second(slice(CHUNK // 2, CHUNK), slice(d_model - 256, d_model))
-            n_copy.wait()
-
-            @pl.when(first & (kind == 1))
-            def _():
-                seed_copy = pltpu.make_async_copy(targets.at[rows], nx, x_sem)
-                seed_copy.start()
-                seed_copy.wait()
-
-                @pl.loop(0, CHUNK // BLK)
-                def _(b):
-                    rb = pl.ds(pl.multiple_of(b * BLK, BLK), BLK)
-                    err = ob[slot, rb].astype(F32) - nx[rb].astype(F32)
-                    ob[slot, rb] = (err * seed_scale).astype(BF)
-                    sse_acc[...] += jnp.sum((err * err).reshape(BLK // 8, 8, d_model), axis=0)
-
-                @pl.when(m == chunks - 1)
-                def _():
-                    acc = sse_acc[:, :128]
-                    for j in range(1, d_model // 128):
-                        acc += sse_acc[:, j * 128:(j + 1) * 128]
-                    sse_sum[...] = acc
-
             for u_copy in u_copies:
                 u_copy.wait()
-            send(kind, m, row, rows, slot)
 
             @pl.when(first & (kind == 1) & (m == chunks - 1))
             def _():
+                acc = sse_acc[:, :128]
+                for j in range(1, d_model // 128):
+                    acc += sse_acc[:, j * 128:(j + 1) * 128]
+                sse_sum[...] = acc
                 for dev in range(1, stages):
                     sse_copy(dev).start()
 
@@ -404,7 +459,7 @@
             for da_copy in da_copies:
                 da_copy.start()
             start_slopes(e_next, (0,))
-            mid_step(s, e, e_next, slot)
+            mid_step(e, e_next, slot, True, True)
             for j in range(d_model // 256 - 1):
                 cols = slice(j * 256, (j + 1) * 256)
                 gt[1, :, cols] = (
@@ -443,29 +498,36 @@
         to = jnp.where(down, jnp.minimum(me + 1, stages - 1), jnp.maximum(me - 1, 0))
         remote = jnp.logical_not(turn | stop)
 
-        @pl.when(remote & (kind < 2))
-        def _():
-            pltpu.make_async_remote_copy(
-                src_ref=ob.at[slot], dst_ref=xs.at[row, rows], send_sem=send_sem.at[slot],
-                recv_sem=recv_sem.at[kind * chunks + m], device_id={'stage': to}).start()
-
         @pl.when(remote & (kind >= 2))
         def _():
             pltpu.make_async_remote_copy(
                 src_ref=ob.at[slot], dst_ref=dhs.at[row, rows], send_sem=send_sem.at[slot],
                 recv_sem=recv_sem.at[kind * chunks + m], device_id={'stage': to}).start()
 
+        @pl.when(turn & (kind == 2))
+        def _():
+            pltpu.make_async_copy(ob.at[slot], dhs.at[0, rows], send_sem.at[slot]).start()
+
+    def send_half(kind, m, row, slot, sub):
+        down = kind == 0
+        turn = (last & down) | (first & (kind == 1))
+        to = jnp.where(down, jnp.minimum(me + 1, stages - 1), jnp.maximum(me - 1, 0))
+        src = ob.at[slot, pl.ds(pl.multiple_of(sub * SUB, SUB), SUB)]
+        place = sub_rows(m, sub)
+
+        @pl.when(jnp.logical_not(turn))
+        def _():
+            pltpu.make_async_remote_copy(
+                src_ref=src, dst_ref=xs.at[row, place], send_sem=send_sem.at[slot],
+                recv_sem=half_sem.at[(kind * chunks + m) * 2 + sub], device_id={'stage': to}).start()
+
         @pl.when(turn & (kind == 0))
         def _():
-            pltpu.make_async_copy(ob.at[slot], xs.at[1, rows], send_sem.at[slot]).start()
+            pltpu.make_async_copy(src, xs.at[1, place], send_sem.at[slot]).start()
 
         @pl.when(turn & (kind == 1))
         def _():
-            pltpu.make_async_copy(ob.at[slot], dhs.at[1, rows], send_sem.at[slot]).start()
-
-        @pl.when(turn & (kind == 2))
-        def _():
-            pltpu.make_async_copy(ob.at[slot], dhs.at[0, rows], send_sem.at[slot]).start()
+            pltpu.make_async_copy(src, dhs.at[1, place], send_sem.at[slot]).start()
 
     lax.fori_loop(0, n_ops, step, 0)
     e_end = entry(jnp.int32(n_ops))
@@ -514,9 +576,9 @@
                 pltpu.VMEM((2, HALVES, d_model, d_ff // HALVES), BF), pltpu.VMEM((2, d_ff, d_model), BF),
                 pltpu.VMEM((2, CHUNK, d_model), BF), pltpu.VMEM((CHUNK, d_model), BF),
                 pltpu.VMEM((HALVES, CHUNK, d_ff // HALVES), BF), pltpu.VMEM((HALVES, CHUNK, d_ff // HALVES), F32),
-                pltpu.VMEM((2, CHUNK, d_model), BF), pltpu.VMEM((8, d_model), F32),
-                pltpu.VMEM((8, 128), F32),
-                pltpu.SemaphoreType.DMA((4 * chunks,)), pltpu.SemaphoreType.DMA((2,)),
+                pltpu.VMEM((2, CHUNK, d_model), BF), pltpu.VMEM((2, SUB, 256), F32),
+                pltpu.VMEM((8, d_model), F32), pltpu.VMEM((8, 128), F32),
+                pltpu.SemaphoreType.DMA((4 * chunks,)), pltpu.SemaphoreType.DMA((4 * chunks,)), pltpu.SemaphoreType.DMA((2,)),
                 pltpu.SemaphoreType.DMA((2,)), pltpu.SemaphoreType.DMA((2 * HALVES + 2,)),
                 pltpu.SemaphoreType.DMA((HALVES + 1,)), pltpu.SemaphoreType.DMA((HALVES,)),
                 pltpu.SemaphoreType.DMA, pltpu.SemaphoreType.DMA((stages,)), pltpu.SemaphoreType.DMA,

time: 1160 us -> 1140 us (0.983)
  Pallas kernels: 910 us -> 893 us
    pallas_call x1, Pallas kernels: 910 us -> 893 us  [device_step(): pl.pallas_call(functools.partial(pipeline_kernel, stages, table, 2.0 / to...]
where the time goes in v3:
time: 1140 us
  Pallas kernels  893 us (78%)
  matrix products  241 us (21%)
    pallas_call x1, Pallas kernels, device_step(): pl.pallas_call(functools.partial(pipeline_kernel, stages, table, 2.0 / to...  893 us
    dot_general x1, matrix products, device_step(): grad_w_out = lax.dot_general(us, dhs, tok, preferred_element_type=F32)  121 us
    dot_general x1, matrix products, device_step(): grad_w_in = lax.dot_general(ns, das, tok, preferred_element_type=F32)  120 us

profile of v3, /device:TPU:0, one launch (start us, length us, event | category | flops | bytes accessed | tf_op | source)
XLA Modules:
  0.0 1139.7 jit_solution(101066447731852197)
XLA Ops:
  0.6 1.3 reshape.22.gains
  1.9 892.7 %vee.1 = (bf16[2,4096,1280]{2,1,0:T(8,128)(2,1)}, bf16[2,4096,1280]{2,1,0:T(8,128)(2,1)}, bf16[2,4096,1280]{2,1,0:T(8,128)(2,1)}, bf16[2,4096,5120]{2,1,0:T(8,12...) custom-call(bf16[4096,1280]{1,0:T(8,128)(2,1)} %bitcast.7, ...), custom_call_target="tpu_custom_call" | custom-call | tf_op jit(solution)/shard_map/vee/pallas_call | solution.py:567
  894.7 1.3 reduce_sum.19
  896.6 0.0 copy-start
  896.6 120.4 %fusion = f32[2,1280,5120]{2,1,0:T(8,128)} fusion(bf16[2,4096,1280]{2,1,0:T(8,128)(2,1)} %get-tuple-element.10, bf16[2,4096,5120]{2,1,0:T(8,128)(2,1)} %get-tuple-element.11), kind=kOutput, calls=%fused_computation | convolution fusion | flops 107374182400 | bytes 157286400 | tf_op jit(solution)/shard_map/dot_general | solution.py:593
  1017.0 0.0 copy-done
  1017.0 0.6 reduce_sum.18
  1017.6 121.0 %fusion.1 = f32[2,5120,1280]{2,1,0:T(8,128)} fusion(bf16[2,4096,5120]{2,1,0:T(8,128)(2,1)} %get-tuple-element.12, bf16[2,4096,1280]{2,1,0:T(8,128)(2,1)} %get-tuple-element.13), kind=kOutput, calls=%fused_computation.1 | convolution fusion | flops 107374182400 | bytes 157286400 | tf_op jit(solution)/shard_map/dot_general | solution.py:594
Async XLA Ops:
  896.6 120.4 %copy-start = (f32[2,8,1280]{2,1,0:T(8,128)S(1)}, f32[2,8,1280]{2,1,0:T(8,128)}, u32[]{:S(2)}) copy-start(f32[2,8,1280]{2,1,0:T(8,128)} %get-tuple-element.14) | copy-start | bytes 245764
